TPU v7x, 32 devices: a whole 2x2x4 slice. The times are simulated.
32 devices in a mesh: gx: 8 (over z, y), gy: 4 (over x, core).
Axes of the slice: x: 2, y: 2, z: 4, core: 2. Of those that a mesh axis runs over, the one named last changes fastest.
Arguments:
- preserved_vector: float32 [14, 64, 32, 128], P(None, 'gx', 'gy'), may hold values from -200 to 200, as said below
- nasa_table: float32 [32, 6], replicated, may hold values from -4 to 4.5, as said below
- gas_constant: float32 [32], replicated, may hold values from 0.3 to 3
- species_index: int32 [9], replicated, may hold values from 0 to 31, as said below
- face_kind: int32 [8, 4, 2], P('gx', 'gy'), may hold values from 0 to 1
Outputs:
- increment: float32 [14, 64, 32, 128], P(None, 'gx', 'gy')
Inputs may be any that keep to these rules, and one draw needn't show every extreme that they name: `preserved_vector`: every cell is a physical state: positive partial densities and an energy whose temperature lies between 0.5 and 2.5. `nasa_table`: each row's cp over R polynomial exceeds 1.5 for temperatures 0.3 to 3. `species_index`: 9 distinct rows.
All inputs are finite; a program needn't handle non-finite values.
Results may differ from a plain program's by a relative error of at most 0.0003.
Values sent between devices are 32-bit elements; how exact they have to be, the bound alone decides.
A program may use at most 64 MiB of HBM per device.

v0:
```python
import jax
import jax.numpy as jnp
from jax import lax
from jax.sharding import PartitionSpec as P

NS = 9
NVAR = 14
NEWTON = 2


EPSILON = 1e-06
COURANT = 0.8


def with_halo(block, sides, width):
    for axis, dim in sides:
        count = lax.axis_size(axis)
        forward = [(i, i + 1) for i in range(count - 1)]
        forward.append((count - 1, 0))
        backward = [(target, source) for source, target in forward]
        low = lax.ppermute(
            lax.slice_in_dim(block, block.shape[dim] - width, None, axis=dim), axis, forward
        )
        high = lax.ppermute(lax.slice_in_dim(block, 0, width, axis=dim), axis, backward)
        block = jnp.concatenate([low, block, high], axis=dim)
    return block


def column(vector, trailing_sizes):
    return vector.reshape((vector.shape[0],) + (1,) * trailing_sizes)


def caloric_fitted_curves_table(nasa_table_weights, kelvin_reading):
    trailing_sizes = kelvin_reading.ndim
    columns = [column(nasa_table_weights[:, degree], trailing_sizes) for degree in range(6)]
    replicated_layer = kelvin_reading[None]
    caloric_quotient = columns[0] + replicated_layer * (
        columns[1]
        + replicated_layer
        * (columns[2] + replicated_layer * (columns[3] + replicated_layer * columns[4]))
    )
    chemical_heat_content = columns[5] + replicated_layer * (
        columns[0]
        + replicated_layer
        * (
            columns[1] / 2.0
            + replicated_layer
            * (
                columns[2] / 3.0
                + replicated_layer * (columns[3] / 4.0 + replicated_layer * columns[4] / 5.0)
            )
        )
    )
    return (caloric_quotient, chemical_heat_content)


def solve_for_kelvin(preserved_vector_lines, nasa_table_weights, component_kind_r_factor):
    prefix_addition_result = preserved_vector_lines[:NS]
    bulk_compactness = jnp.sum(prefix_addition_result, axis=0)
    momentum = preserved_vector_lines[NS : NS + 3]
    caloric_content_inner = (
        preserved_vector_lines[NS + 3]
        - 0.5 * jnp.sum(momentum * momentum, axis=0) / bulk_compactness
    )
    blend_stack_lane = column(component_kind_r_factor, bulk_compactness.ndim)
    kelvin_reading = jnp.ones_like(bulk_compactness)
    for iteration in range(NEWTON):
        caloric_quotient, chemical_heat_content = caloric_fitted_curves_table(
            nasa_table_weights, kelvin_reading
        )
        solver_misfit = (
            jnp.sum(
                prefix_addition_result
                * blend_stack_lane
                * (chemical_heat_content - kelvin_reading[None]),
                axis=0,
            )
            - caloric_content_inner
        )
        tangent_steepness_fn = jnp.sum(
            prefix_addition_result * blend_stack_lane * (caloric_quotient - 1.0), axis=0
        )
        kelvin_reading = kelvin_reading - solver_misfit / tangent_steepness_fn
    return kelvin_reading


def nasa_fitted_monomials(
    preserved_vector_lines, kelvin_reading, nasa_table_weights, component_kind_r_factor
):
    prefix_addition_result = preserved_vector_lines[:NS]
    bulk_compactness = jnp.sum(prefix_addition_result, axis=0)
    momentum = preserved_vector_lines[NS : NS + 3]
    doubled_norm_motion = jnp.sum(momentum * momentum, axis=0) / (
        bulk_compactness * bulk_compactness
    )
    blend_stack_lane = column(component_kind_r_factor, bulk_compactness.ndim)
    caloric_quotient, chemical_heat_content = caloric_fitted_curves_table(
        nasa_table_weights, kelvin_reading
    )
    caloric_tiers = blend_stack_lane * (chemical_heat_content - kelvin_reading[None])
    averaged_mixing_law_r = jnp.sum(prefix_addition_result * blend_stack_lane, axis=0)
    thrust_load_quiet = averaged_mixing_law_r * kelvin_reading
    heat_quotient_decrement = averaged_mixing_law_r / jnp.sum(
        prefix_addition_result * blend_stack_lane * (caloric_quotient - 1.0), axis=0
    )
    sound_speed = jnp.sqrt((1.0 + heat_quotient_decrement) * thrust_load_quiet / bulk_compactness)
    force_spatial_jump = (
        blend_stack_lane * kelvin_reading[None]
        - heat_quotient_decrement[None] * caloric_tiers
        + 0.5 * heat_quotient_decrement[None] * doubled_norm_motion[None]
    )
    return jnp.concatenate(
        [
            thrust_load_quiet[None],
            heat_quotient_decrement[None],
            sound_speed[None],
            force_spatial_jump,
        ],
        axis=0,
    )


def reconstruct(values):
    value_zero, value_one, value_two, value_three, value_four = values
    candidate_zero = (2.0 * value_zero - 7.0 * value_one + 11.0 * value_two) / 6.0
    candidate_one = (-value_one + 5.0 * value_two + 2.0 * value_three) / 6.0
    candidate_two = (2.0 * value_two + 5.0 * value_three - value_four) / 6.0
    curve_zero = value_zero - 2.0 * value_one + value_two
    slope_zero = value_zero - 4.0 * value_one + 3.0 * value_two
    curve_one = value_one - 2.0 * value_two + value_three
    slope_one = value_one - value_three
    curve_two = value_two - 2.0 * value_three + value_four
    slope_two = 3.0 * value_two - 4.0 * value_three + value_four
    smooth_zero = 13.0 / 12.0 * curve_zero * curve_zero + 0.25 * slope_zero * slope_zero
    smooth_one = 13.0 / 12.0 * curve_one * curve_one + 0.25 * slope_one * slope_one
    smooth_two = 13.0 / 12.0 * curve_two * curve_two + 0.25 * slope_two * slope_two
    weight_zero = 0.1 / ((EPSILON + smooth_zero) * (EPSILON + smooth_zero))
    weight_one = 0.6 / ((EPSILON + smooth_one) * (EPSILON + smooth_one))
    weight_two = 0.3 / ((EPSILON + smooth_two) * (EPSILON + smooth_two))
    return (
        weight_zero * candidate_zero + weight_one * candidate_one + weight_two * candidate_two
    ) / (weight_zero + weight_one + weight_two)


def window(array, offset, count, array_axis):
    return lax.slice_in_dim(array, offset, offset + count, axis=array_axis)


def direction_rate(preserved_vector_lines, cell_coef, array_axis, normal, speed):
    cells = preserved_vector_lines.shape[array_axis] - 6
    faces = cells + 1
    bulk_compactness = jnp.sum(preserved_vector_lines[:NS], axis=0)
    fractions = preserved_vector_lines[:NS] / bulk_compactness[None]
    velocity = preserved_vector_lines[NS : NS + 3] / bulk_compactness[None]
    passive = preserved_vector_lines[NS + 4 : NS + 5] / bulk_compactness[None]
    thrust_load_quiet = cell_coef[0]
    normal_speed = velocity[normal]
    carried = preserved_vector_lines * normal_speed[None]
    flux_rows = [carried[:NS]]
    for component in range(3):
        if component == normal:
            flux_rows.append((carried[NS + component] + thrust_load_quiet)[None])
        else:
            flux_rows.append(carried[NS + component][None])
    flux_rows.append((carried[NS + 3] + thrust_load_quiet * normal_speed)[None])
    flux_rows.append(carried[NS + 4][None])
    physical = jnp.concatenate(flux_rows, axis=0)
    upwind = 0.5 * (physical + speed * preserved_vector_lines)
    downwind = 0.5 * (physical - speed * preserved_vector_lines)

    def average(array):
        return 0.5 * (window(array, 2, faces, array_axis) + window(array, 3, faces, array_axis))

    mean_frac = average(fractions)
    mean_vel = average(velocity)
    mean_passive = average(passive)[0]
    mean_gamma = average(cell_coef[1:2])[0]
    mean_sound = average(cell_coef[2:3])[0]
    mean_slopes = average(cell_coef[3:])
    mean_square = jnp.sum(mean_vel * mean_vel, axis=0)
    mean_enthalpy = (
        mean_sound * mean_sound - jnp.sum(mean_frac * mean_slopes, axis=0)
    ) / mean_gamma + mean_square
    inverse = 1.0 / (mean_sound * mean_sound)
    tangents = [component for component in range(3) if component != normal]

    def project(vector):
        total = jnp.sum(vector[:NS], axis=0)
        pressure_jump = (
            jnp.sum(mean_slopes * vector[:NS], axis=0)
            - mean_gamma * jnp.sum(mean_vel * vector[NS : NS + 3], axis=0)
            + mean_gamma * vector[NS + 3]
        )
        normal_jump = vector[NS + normal] - mean_vel[normal] * total
        scaled = pressure_jump * inverse
        slower = 0.5 * (pressure_jump - mean_sound * normal_jump) * inverse
        faster = 0.5 * (pressure_jump + mean_sound * normal_jump) * inverse
        species = vector[:NS] - mean_frac * scaled[None]
        first_shear = vector[NS + tangents[0]] - mean_vel[tangents[0]] * total
        second_shear = vector[NS + tangents[1]] - mean_vel[tangents[1]] * total
        scalar_wave = vector[NS + 4] - mean_passive * scaled
        return jnp.concatenate(
            [
                slower[None],
                species,
                first_shear[None],
                second_shear[None],
                faster[None],
                scalar_wave[None],
            ],
            axis=0,
        )

    rising = reconstruct(
        [project(window(upwind, offset, faces, array_axis)) for offset in (0, 1, 2, 3, 4)]
    )
    falling = reconstruct(
        [project(window(downwind, offset, faces, array_axis)) for offset in (5, 4, 3, 2, 1)]
    )
    amplitude = rising + falling
    slower = amplitude[0]
    species = amplitude[1 : NS + 1]
    first_shear = amplitude[NS + 1]
    second_shear = amplitude[NS + 2]
    faster = amplitude[NS + 3]
    scalar_wave = amplitude[NS + 4]
    species_total = jnp.sum(species, axis=0)
    acoustic = slower + faster
    normal_vel = mean_vel[normal]
    momentum_rows = []
    for component in range(3):
        if component == normal:
            momentum_rows.append(
                (normal_vel - mean_sound) * slower
                + (normal_vel + mean_sound) * faster
                + normal_vel * species_total
            )
        elif component == tangents[0]:
            momentum_rows.append(mean_vel[component] * (acoustic + species_total) + first_shear)
        else:
            momentum_rows.append(mean_vel[component] * (acoustic + species_total) + second_shear)
    energy_row = (
        (mean_enthalpy - normal_vel * mean_sound) * slower
        + (mean_enthalpy + normal_vel * mean_sound) * faster
        + jnp.sum((mean_square[None] - mean_slopes / mean_gamma[None]) * species, axis=0)
        + mean_vel[tangents[0]] * first_shear
        + mean_vel[tangents[1]] * second_shear
    )
    face_flux = jnp.concatenate(
        [
            mean_frac * acoustic[None] + species,
            jnp.stack(momentum_rows, axis=0),
            energy_row[None],
            (mean_passive * acoustic + scalar_wave)[None],
        ],
        axis=0,
    )
    return window(face_flux, 0, cells, array_axis) - window(face_flux, 1, cells, array_axis)


def wall_pad(payload, lower_kind, upper_kind):
    rows_count = payload.shape[0]
    sign_flips = (
        jnp.where(jnp.arange(rows_count) == NS + 2, -1.0, 1.0)
        .astype(payload.dtype)
        .reshape((rows_count, 1, 1, 1))
    )
    lower_copy = jnp.concatenate([payload[..., :1]] * 3, axis=3)
    upper_copy = jnp.concatenate([payload[..., -1:]] * 3, axis=3)
    lower_mirror = payload[..., 2::-1] * sign_flips
    upper_mirror = payload[..., :-4:-1] * sign_flips
    lower_ghost = jnp.where(lower_kind == 1, lower_mirror, lower_copy)
    upper_ghost = jnp.where(upper_kind == 1, upper_mirror, upper_copy)
    return jnp.concatenate([lower_ghost, payload, upper_ghost], axis=3)


def fill_rims(padded):
    preserved_vector_lines = padded[:NVAR]
    return (preserved_vector_lines, padded[NVAR:])


def shards(preserved_vector, nasa_table, gas_constant, species_index, face_kind):
    selector = (
        species_index[:, None] == jnp.arange(nasa_table.shape[0], dtype=jnp.int32)[None, :]
    ).astype(jnp.float32)
    nasa_table_weights = jnp.dot(selector, nasa_table, precision=lax.Precision.HIGHEST)
    component_kind_r_factor = jnp.dot(
        selector, gas_constant[:, None], precision=lax.Precision.HIGHEST
    )[:, 0]
    kelvin_reading = solve_for_kelvin(preserved_vector, nasa_table_weights, component_kind_r_factor)
    self_coefficient = nasa_fitted_monomials(
        preserved_vector, kelvin_reading, nasa_table_weights, component_kind_r_factor
    )
    bulk_compactness = jnp.sum(preserved_vector[:NS], axis=0)
    velocity = preserved_vector[NS : NS + 3] / bulk_compactness[None]
    local_speed = jnp.max(jnp.abs(velocity) + self_coefficient[2][None], axis=(1, 2, 3))
    speeds = lax.pmax(local_speed, ("gx", "gy"))
    joined = jnp.concatenate([preserved_vector, self_coefficient], axis=0)
    padded_x = with_halo(joined, (("gx", 1),), 3)
    padded_y = with_halo(joined, (("gy", 2),), 3)
    padded_z = wall_pad(joined, face_kind[0, 0, 0], face_kind[0, 0, 1])
    rate = direction_rate(padded_z[:NVAR], padded_z[NVAR:], 3, 2, speeds[2])
    state_x, coef_x = fill_rims(padded_x)
    rate = rate + direction_rate(state_x, coef_x, 1, 0, speeds[0])
    state_y, coef_y = fill_rims(padded_y)
    rate = rate + direction_rate(state_y, coef_y, 2, 1, speeds[1])
    return COURANT / jnp.sum(speeds) * rate


def solution(mesh):
    return jax.shard_map(
        shards,
        mesh=mesh,
        in_specs=(P(None, "gx", "gy", None), P(), P(), P(), P("gx", "gy", None)),
        out_specs=P(None, "gx", "gy", None),
        check_vma=False,
    )
```

profile of v0, /device:TPU:0, one launch (start us, length us, event | category | flops | bytes accessed | tf_op | source)
XLA Modules:
  0.0 107.5 jit_solution(1922939671895557991)
XLA Ops:
  0.0 0.7 copy-done
  0.7 0.8 fusion.278
  1.6 1.1 constant_dynamic-update-slice_fusion.4
  2.6 0.9 multiply_reduce_fusion.41
  3.5 0.9 convolution_bitcast_fusion
  4.4 1.1 %multiply_reduce_fusion.37 = (f32[8,8,128]{2,1,0:T(8,128)S(1)}, f32[8,8,128]{2,1,0:T(8,128)S(1)}, f32[8,8,128]{2,1,0:T(8,128)S(1)}) fusion(f32[9]{0:T(128)S(1)} %get-tuple-element.625, f32[9]{0:T(128)S(1)} %convolution_bitcast_fusion, f32[14,8,8,128]{3,2,1,0:T(8,128)} %param.5, f32[9]{0:T(128)S(1)} %get-tuple-element.621), kind=kLoop, calls=%fused_computation.473 | loop fusion | flops 417792 | bytes 393324 | tf_op jit(solution)/shard_map/reduce_sum | solution.py:72
  5.5 0.3 fusion.124
  5.9 0.2 fusion.122
  6.2 0.6 constant_dynamic-update-slice_fusion.1
  6.8 0.2 constant_dynamic-update-slice_fusion
  7.1 0.9 fusion.363
  7.9 6.0 %collective-permute-start.1 = (f32[26,3,8,128]{3,2,1,0:T(8,128)}, f32[26,3,8,128]{3,2,1,0:T(8,128)S(1)}, u32[]{:S(2)}, u32[]{:S(2)}) collective-permute-start(f32[26,3,8,128]{3,2,1,0:T(8,128)} %get-tuple-element.536), channel_id=1, source_target_pairs={{4,0},{8,4},{12,8},{16,12},{20,16},{24,20},{28,24},{0,28},{5,1},{9... | collective-permute-start | bytes 958472 | tf_op jit(solution)/shard_map/ppermute | solution.py:24
  14.0 0.2 fusion.360
  14.2 0.8 copy.907
  15.0 0.8 copy.908
  15.7 1.7 %collective-permute-start.3 = (f32[26,8,3,128]{3,1,2,0:T(8,128)}, f32[26,8,3,128]{3,1,2,0:T(8,128)}, u32[]{:S(2)}, u32[]{:S(2)}) collective-permute-start(f32[26,8,3,128]{3,1,2,0:T(8,128)} %copy.908), channel_id=1, source_target_pairs={{1,0},{2,1},{3,2},{0,3},{5,4},{6,5},{7,6},{4,7},{9,8},{10,9},{11,1... | collective-permute-start | bytes 958472 | tf_op jit(solution)/shard_map/ppermute | solution.py:24
  17.5 1.2 %fusion.362 = (f32[26,8,8,3]{3,2,1,0:T(8,128)}, f32[26,8,8,3]{3,2,1,0:T(8,128)S(1)}) fusion(f32[26,8,8,128]{3,2,1,0:T(8,128)S(1)} %constant_dynamic-update-slice_fusion), kind=kLoop, calls=%fused_computation.1076 | loop fusion | bytes 79872 | tf_op jit(solution)/shard_map/slice | solution.py:270
  18.7 1.2 %fusion.361 = (f32[26,8,8,1]{3,2,1,0:T(8,128)}, f32[26,8,8,1]{3,2,1,0:T(8,128)S(1)}) fusion(f32[26,8,8,128]{3,2,1,0:T(8,128)S(1)} %constant_dynamic-update-slice_fusion), kind=kLoop, calls=%fused_computation.1075 | loop fusion | bytes 26624 | tf_op jit(solution)/shard_map/slice | solution.py:268
  19.9 2.2 %rev.6 = f32[26,8,8,3]{3,2,1,0:T(8,128)} reverse(f32[26,8,8,3]{3,2,1,0:T(8,128)} %get-tuple-element.533), dimensions={3} | reverse | bytes 39936 | tf_op jit(solution)/shard_map/rev | solution.py:270
  22.0 2.4 %copy.898 = f32[26,8,8,1]{2,1,0,3:T(8,128)S(1)} copy(f32[26,8,8,1]{3,2,1,0:T(8,128)} %get-tuple-element.531) | data formatting | bytes 13312 | tf_op jit(solution)/shard_map/slice | solution.py:268
  24.5 0.7 fusion.366
  25.1 1.3 %copy.899 = f32[26,8,8,1]{2,1,0,3:T(8,128)S(1)} copy(f32[26,8,8,1]{3,2,1,0:T(8,128)S(1)} %get-tuple-element.532) | data formatting | bytes 13312 | tf_op jit(solution)/shard_map/slice | solution.py:269
  26.4 1.2 %rev.7 = f32[26,8,8,3]{3,2,1,0:T(8,128)} reverse(f32[26,8,8,3]{3,2,1,0:T(8,128)S(1)} %get-tuple-element.534), dimensions={3} | reverse | bytes 39936 | tf_op jit(solution)/shard_map/rev | solution.py:271
  29.0 1.9 %multiply_select_fusion.1 = (f32[26,8,8,3]{3,2,1,0:T(8,128)S(1)}, f32[26,8,8,3]{3,2,1,0:T(8,128)S(1)}) fusion(f32[26,8,8,3]{3,2,1,0:T(8,128)} %rev.6, f32[26,8,8]{2,1,0:T(8,128)S(1)} %bitcast.929, f32[26]{0:T(128)S(1)} %compare_select_fusion, pred[]{:T(512)} %bitcast.19, f32[26,8,8]{2,1,0:T(8,128)S(1)} %bitcast.930, f32[26,8,8,3]{3,2,1,0:T(8,128)} %rev.7, ...), kind=kLoop, calls=%fused_computation.54 | loop fusion | flops 19968 | bytes 93290 | tf_op jit(solution)/shard_map/jit(_where)/select_n | solution.py:272
  30.9 0.7 pad_maximum_fusion
  31.7 0.1 maximum_divide_fusion
  31.9 1.1 slice_divide_fusion
  33.0 1.0 add_reduce_fusion
  34.1 0.9 slice_add_fusion.10
  35.0 0.9 slice.1842
  36.0 40.2 %pmax.7 = f32[3]{0:T(128)S(1)} all-reduce(f32[3]{0:T(128)S(1)} %add_reduce_fusion), channel_id=1, replica_groups=mesh['gx'=8,'gy'=4] {'gx','gy'}, use_global_device_ids=true, to_apply=%region_9.0 | all-reduce | flops 3 | bytes 24 | tf_op jit(solution)/shard_map/pmax | solution.py:297
  76.1 0.6 fusion.365
  76.7 0.9 slice_add_fusion.9
  77.6 2.3 %subtract_multiply_fusion = (f32[14,8,8,134]{3,2,1,0:T(8,128)S(1)}, f32[14,8,8,134]{3,2,1,0:T(8,128)S(1)}) fusion(f32[26,8,8,134]{3,2,1,0:T(8,128)} %copy-done.2, f32[1,8,8,134]{3,2,1,0:T(8,128)} %get-tuple-element.438, f32[1,8,8,134]{3,2,1,0:T(8,128)S(1)} %slice_add_fusion.9, f32[1,8,8,134]{3,2,1,0:T(8,128)S(1)} %get-tuple-element.262, ...), kind=kLoop, calls=%fused_computation.49 | loop fusion | flops 960512 | bytes 1921028 | tf_op jit(solution)/shard_map/mul | solution.py:169
  79.9 0.9 slice_reduce_fusion.11
  80.8 0.6 fusion.134
  81.6 0.1 multiply_bitcast_fusion.9
  81.8 0.9 copy-done.4
  82.7 0.4 subtract_dynamic-update-slice_fusion.9
  83.1 0.1 constant_dynamic-update-slice_fusion.14
  83.2 1.4 %subtract_dynamic-update-slice_fusion.8 = (f32[14,8,8,129]{3,2,1,0:T(8,128)S(1)}, f32[14,8,8,129]{3,2,1,0:T(8,128)S(1)}, f32[14,8,8,129]{3,2,1,0:T(8,128)S(1)}, ...) fusion(f32[14,8,8,129]{3,2,1,0:T(8,128)S(1)} %get-tuple-element, ...), kind=kLoop, calls=%fused_computation.111 | loop fusion | flops 1841088 | bytes 9830400
  84.7 0.2 multiply_bitcast_fusion.5
  84.9 0.2 constant_dynamic-update-slice_fusion.34
  85.1 0.8 subtract_dynamic-update-slice_fusion.4
  86.4 0.1 constant_dynamic-update-slice_fusion.33
  86.8 0.1 constant_dynamic-update-slice_fusion.10
  87.0 0.2 constant_dynamic-update-slice_fusion.30
  87.1 4.1 %divide_add_fusion = f32[14,8,8,129]{3,2,1,0:T(8,128)S(1)} fusion(f32[14,8,8,129]{3,2,1,0:T(8,128)S(1)} %get-tuple-element.402, f32[14,8,8,129]{3,2,1,0:T(8,128)S(1)} %get-tuple-element.400, f32[14,8,8,129]{3,2,1,0:T(8,128)S(1)} %get-tuple-element.401, f32[14,8,8,129]{3,2,1,0:T(8,128)S(1)} %get-tuple-element.403, ...), kind=kLoop, calls=%fused_computation.48 | loop fusion | flops 14910336 | bytes 5085696 | tf_op jit(solution)/shard_map/add | solution.py:220
  91.3 0.2 multiply_reduce_fusion
  91.7 0.7 reduce_sum.1271
  93.1 1.0 constant_dynamic-update-slice_fusion.134
  94.1 0.2 constant_dynamic-update-slice_fusion.133
  94.4 1.0 constant_dynamic-update-slice_fusion.135
  96.0 0.8 subtract_multiply_fusion.2
  96.9 0.2 slice_reduce_fusion.35
  97.3 0.3 constant_dynamic-update-slice_fusion.74
  97.8 0.2 constant_dynamic-update-slice_fusion.98
  98.3 2.6 %divide_add_fusion.2 = f32[14,9,8,128]{3,2,1,0:T(8,128)S(1)} fusion(f32[14,9,8,128]{3,2,1,0:T(8,128)S(1)} %get-tuple-element.516, f32[14,9,8,128]{3,2,1,0:T(8,128)S(1)} %get-tuple-element.514, f32[14,9,8,128]{3,2,1,0:T(8,128)S(1)} %get-tuple-element.515, f32[14,9,8,128]{3,2,1,0:T(8,128)S(1)} %get-tuple-element.517, ...), kind=kLoop, calls=%fused_computation.179 | loop fusion | flops 16644096 | bytes 5677056 | tf_op jit(solution)/shard_map/add | solution.py:220
  101.3 0.8 subtract_multiply_fusion.1
  102.2 0.2 slice_reduce_fusion.24
  102.7 0.4 constant_dynamic-update-slice_fusion.151
  103.2 0.1 constant_dynamic-update-slice_fusion.175
  103.7 2.3 %divide_add_fusion.1 = f32[14,8,9,128]{3,1,2,0:T(8,128)S(1)} fusion(f32[14,8,9,128]{3,1,2,0:T(8,128)S(1)} %get-tuple-element.493, f32[14,8,9,128]{3,1,2,0:T(8,128)S(1)} %get-tuple-element.491, f32[14,8,9,128]{3,1,2,0:T(8,128)S(1)} %get-tuple-element.492, f32[14,8,9,128]{3,1,2,0:T(8,128)S(1)} %get-tuple-element.494, ...), kind=kLoop, calls=%fused_computation.178 | loop fusion | flops 16644096 | bytes 5677056 | tf_op jit(solution)/shard_map/add | solution.py:220
  106.3 1.1 %fusion.78 = f32[14,8,8,128]{3,2,1,0:T(8,128)} fusion(f32[14,9,8,128]{3,2,1,0:T(8,128)S(1)} %constant_dynamic-update-slice_fusion.124, f32[14,8,8,129]{3,2,1,0:T(8,128)S(1)} %constant_dynamic-update-slice_fusion.55, f32[14,8,8,128]{3,1,2,0:T(8,128)S(1)} %get-tuple-element.553, f32[14,8,8,128]{3,1,2,0:T(8,128)S(1)} %get-tuple-element.552, f32[]{:T(128)S(6)} %div.468), kind=kLoop, calls=%fused_computation.187 | loop fusion | flops 688128 | bytes 3211268 | tf_op jit(solution)/shard_map/mul | solution.py:307
  (118 shorter events, 4.2 us)
Async XLA Ops:
  0.0 0.7 copy-start
  0.0 5.5 %copy-start.3 = (f32[14,8,8,128]{3,2,1,0:T(8,128)S(1)}, f32[14,8,8,128]{3,2,1,0:T(8,128)}, u32[]{:S(2)}) copy-start(f32[14,8,8,128]{3,2,1,0:T(8,128)} %param.5) | copy-start | bytes 1376260
  7.9 87.6 %collective-permute-start.1 = (f32[26,3,8,128]{3,2,1,0:T(8,128)}, f32[26,3,8,128]{3,2,1,0:T(8,128)S(1)}, u32[]{:S(2)}, u32[]{:S(2)}) collective-permute-start(f32[26,3,8,128]{3,2,1,0:T(8,128)} %get-tuple-element.536), channel_id=1, source_target_pairs={{4,0},{8,4},{12,8},{16,12},{20,16},{24,20},{28,24},{0,28},{5,1},{9... | collective-permute-start | bytes 958472 | tf_op jit(solution)/shard_map/ppermute | solution.py:24
  14.0 81.5 %collective-permute-start = (f32[26,3,8,128]{3,2,1,0:T(8,128)}, f32[26,3,8,128]{3,2,1,0:T(8,128)S(1)}, u32[]{:S(2)}, u32[]{:S(2)}) collective-permute-start(f32[26,3,8,128]{3,2,1,0:T(8,128)} %get-tuple-element.535), channel_id=1, source_target_pairs={{0,4},{4,8},{8,12},{12,16},{16,20},{20,24},{24,28},{28,0},{1,5},{5... | collective-permute-start | bytes 958472 | tf_op jit(solution)/shard_map/ppermute | solution.py:21
  15.0 78.1 %collective-permute-start.2 = (f32[26,8,3,128]{3,1,2,0:T(8,128)}, f32[26,8,3,128]{3,1,2,0:T(8,128)}, u32[]{:S(2)}, u32[]{:S(2)}) collective-permute-start(f32[26,8,3,128]{3,1,2,0:T(8,128)} %copy.907), channel_id=1, source_target_pairs={{0,1},{1,2},{2,3},{3,0},{4,5},{5,6},{6,7},{7,4},{8,9},{9,10},{10,1... | collective-permute-start | bytes 958472 | tf_op jit(solution)/shard_map/ppermute | solution.py:21
  15.7 78.6 %collective-permute-start.3 = (f32[26,8,3,128]{3,1,2,0:T(8,128)}, f32[26,8,3,128]{3,1,2,0:T(8,128)}, u32[]{:S(2)}, u32[]{:S(2)}) collective-permute-start(f32[26,8,3,128]{3,1,2,0:T(8,128)} %copy.908), channel_id=1, source_target_pairs={{1,0},{2,1},{3,2},{0,3},{5,4},{6,5},{7,6},{4,7},{9,8},{10,9},{11,1... | collective-permute-start | bytes 958472 | tf_op jit(solution)/shard_map/ppermute | solution.py:24
  19.9 4.6 %copy-start.7 = (s32[1,1,2]{2,1,0:T(1,128)S(1)}, s32[1,1,2]{2,1,0:T(1,128)}, u32[]{:S(2)}) copy-start(s32[1,1,2]{2,1,0:T(1,128)} %param.9) | copy-start | bytes 28
  31.7 2.3 %copy-start.2 = (f32[26,8,8,134]{3,2,1,0:T(8,128)}, f32[26,8,8,134]{3,2,1,0:T(8,128)S(1)}, u32[]{:S(2)}) copy-start(f32[26,8,8,134]{3,2,1,0:T(8,128)S(1)} %pad_maximum_fusion) | copy-start | bytes 2675716
  31.7 1.2 %copy-start.6 = (f32[1,8,8,128]{3,2,1,0:T(8,128)S(1)}, f32[1,8,8,128]{3,2,1,0:T(8,128)}, u32[]{:S(2)}) copy-start(f32[1,8,8,128]{3,2,1,0:T(8,128)} %get-tuple-element.319) | copy-start | bytes 98308
  34.1 1.0 copy-start.5
  81.6 1.1 copy-start.4
  106.3 1.1 %copy-start.1 = (f32[32,6]{0,1:T(8,128)S(1)}, f32[32,6]{0,1:T(8,128)}, u32[]{:S(2)}) copy-start(f32[32,6]{0,1:T(8,128)} %param.6) | copy-start | bytes 2308
where the time goes:
time: 108 us; the launch traced here: 107 us
  blocking collectives  40.2 us (37%)
  other arithmetic  35.4 us (33%)
  local copies, waits for them, and re-layouts  19.5 us (18%)
  starting transfers between devices  7.78 us (7%)
  between operations  2.88 us (3%)
  matrix products  1.7 us (2%)
    pmax x1, blocking collectives, shards(): speeds = lax.pmax(local_speed, ('gx', 'gy'))  40.2 us
    add x3, other arithmetic, direction_rate(): amplitude = rising + falling  9.05 us
    ppermute x2, starting transfers between devices, with_halo(): lax.ppermute(lax.slice_in_dim(block, 0, width, axis=dim), axis, backward)  7.78 us
    unnamed x57, other arithmetic  6.56 us
    unnamed x24, local copies, waits for them, and re-layouts  5.37 us
    mul x3, other arithmetic, direction_rate(): downwind = 0.5 * (physical - speed * preserved_vector_lines)  3.87 us
    slice x2, local copies, waits for them, and re-layouts, wall_pad(): lower_copy = jnp.concatenate([payload[..., :1]] * 3, axis=3)  3.59 us
    rev x1, local copies, waits for them, and re-layouts, wall_pad(): lower_mirror = payload[..., 2::-1] * sign_flips  2.18 us
  transfers between devices with their start and end apart: 4, of which 0 were waited for; matrix products, arithmetic and copies ran while one was open for 34% of the time, Pallas kernels for 0%

commit v1 on v0

v1 whole, which is shorter than its diff:
```python
import functools

import jax
import jax.numpy as jnp
from jax import lax
from jax.experimental import pallas as pl
from jax.experimental.pallas import tpu as pltpu
from jax.sharding import PartitionSpec as P

NS = 9
NVAR = 14
EPSILON = 1e-06
COURANT = 0.8
TOTAL = NVAR
PRIMS = 24
VEL, PASSIVE, GAMMA, SOUND, SLOPES = 9, 12, 13, 14, 15
TABLE = 7 * NS


def fill_table(nasa_ref, gas_ref, index_ref, table_ref):
    for i in range(NS):
        row = index_ref[i]
        gas = gas_ref[row]
        values = [
            gas,
            gas * nasa_ref[row, 5],
            gas * (nasa_ref[row, 0] - 1.0),
            gas * nasa_ref[row, 1] * (1.0 / 2.0),
            gas * nasa_ref[row, 2] * (1.0 / 3.0),
            gas * nasa_ref[row, 3] * (1.0 / 4.0),
            gas * nasa_ref[row, 4] * (1.0 / 5.0),
        ]
        for n, value in enumerate(values):
            table_ref[n * NS + i] = jnp.full(table_ref.shape[1:], value, jnp.float32)


def tree(terms):
    terms = list(terms)
    while len(terms) > 1:
        terms = [a + b for a, b in zip(terms[::2], terms[1::2])] + (
            [terms[-1]] if len(terms) % 2 else []
        )
    return terms[0]


def thermo(u, table_ref):
    rho = tree(u[:NS])
    inverse = 1.0 / rho
    vel = [m * inverse for m in u[NS : NS + 3]]
    square = tree([v * v for v in vel])
    inner = u[NS + 3] - 0.5 * tree([v * m for v, m in zip(vel, u[NS : NS + 3])])
    mix = [tree([u[i] * table_ref[n * NS + i] for i in range(NS)]) for n in range(7)]
    gas, m6, m1, m2, m3, m4, m5 = mix
    c2, c3, c4, c5 = 2.0 * m2, 3.0 * m3, 4.0 * m4, 5.0 * m5
    temp = 1.0 - (tree([m6, m1, m2, m3, m4, m5]) - inner) / tree([m1, c2, c3, c4, c5])

    def heat(t):
        return m1 + t * (c2 + t * (c3 + t * (c4 + t * c5)))

    energy = m6 + temp * (m1 + temp * (m2 + temp * (m3 + temp * (m4 + temp * m5))))
    temp = temp - (energy - inner) / heat(temp)
    pressure = temp * gas
    gamma = gas / heat(temp)
    sound = jnp.sqrt((1.0 + gamma) * pressure * inverse)
    return inverse, vel, square, temp, pressure, gamma, sound


def slopes_of(temp, gamma, square, table_ref):
    kinetic = 0.5 * gamma * square
    result = []
    for i in range(NS):
        k = [table_ref[n * NS + i] for n in range(7)]
        e = k[1] + temp * (k[2] + temp * (k[3] + temp * (k[4] + temp * (k[5] + temp * k[6]))))
        result.append(k[0] * temp - gamma * e + kinetic)
    return result


def reciprocal(x):
    return pl.reciprocal(x, approx=True)


def correction(d):
    d0, d1, d2, d3 = d
    e0, e1, e2 = d1 - d0, d2 - d1, d3 - d2
    h1, h2 = 0.75 * d1, 0.75 * d2
    near, far = h1 * d1 + 0.75 * EPSILON, h2 * d2 + 0.75 * EPSILON
    r0 = reciprocal(e0 * (e0 + h1) + near)
    r1 = reciprocal(e1 * (e1 + h1) + near)
    r2 = reciprocal(e2 * (e2 - h2) + far)
    a = r0 * r0 * (1.0 / 3.0)
    b = r1 * r1
    c = r2 * r2
    g0, g2 = e0 - e1, e1 - e2
    return (a * (g0 + g0) + c * g2) * reciprocal(a + c + (b + b))


def face(normal, up, down, mean, linear, put):
    phi = [mean(SLOPES + i) for i in range(NS)]
    vel = [mean(VEL + i) for i in range(3)]
    gamma, sound = mean(GAMMA), mean(SOUND)
    inv = 1.0 / sound
    inv2, half_inv = inv * inv, 0.5 * inv
    tangents = [t for t in range(3) if t != normal]
    sigma, slow, fast = ([], []), ([], []), ([], [])
    shear = [([], []), ([], [])]
    for side, get in enumerate((up, down)):
        for k in range(4):
            s = get(TOTAL, k)
            m = [get(NS + i, k) for i in range(3)]
            dp = tree([phi[i] * get(i, k) for i in range(NS)]) + gamma * (
                get(NS + 3, k) - tree([vel[i] * m[i] for i in range(3)])
            )
            scaled = dp * inv2
            jump = (m[normal] - vel[normal] * s) * half_inv
            half = 0.5 * scaled
            sigma[side].append(scaled)
            slow[side].append(half - jump)
            fast[side].append(half + jump)
            for n, t in enumerate(tangents):
                shear[n][side].append(m[t] - vel[t] * s)

    def both(pair):
        return correction(pair[0]) - correction(pair[1])

    slower, faster = both(slow), both(fast)
    shears = [both(pair) for pair in shear]
    acoustic = slower + faster
    total, weighted, blend = None, None, None
    for i in range(NS):
        y = mean(i)
        amp = both(
            (
                [up(i, k) - y * sigma[0][k] for k in range(4)],
                [down(i, k) - y * sigma[1][k] for k in range(4)],
            )
        )
        put(i, linear(i) + y * acoustic + amp)
        total = amp if i == 0 else total + amp
        weighted = phi[i] * amp if i == 0 else weighted + phi[i] * amp
        blend = phi[i] * y if i == 0 else blend + phi[i] * y
    z = mean(PASSIVE)
    amp = both(
        (
            [up(NS + 4, k) - z * sigma[0][k] for k in range(4)],
            [down(NS + 4, k) - z * sigma[1][k] for k in range(4)],
        )
    )
    put(NS + 4, linear(NS + 4) + z * acoustic + amp)
    mass = acoustic + total
    swing = sound * (faster - slower)
    put(NS + normal, linear(NS + normal) + vel[normal] * mass + swing)
    for n, t in enumerate(tangents):
        put(NS + t, linear(NS + t) + vel[t] * mass + shears[n])
    square = tree([v * v for v in vel])
    energy = (
        square * mass
        + ((sound * sound - blend) * acoustic - weighted) / gamma
        + vel[normal] * swing
        + vel[tangents[0]] * shears[0]
        + vel[tangents[1]] * shears[1]
    )
    put(NS + 3, linear(NS + 3) + energy)


def fill_cells(u, i, table_ref, prim_ref):
    inverse, vel, square, temp, pressure, gamma, sound = thermo(u, table_ref)
    for k in range(NS):
        prim_ref[k, i] = u[k] * inverse
    for k in range(3):
        prim_ref[VEL + k, i] = vel[k]
    prim_ref[PASSIVE, i] = u[NS + 4] * inverse
    prim_ref[GAMMA, i] = gamma
    prim_ref[SOUND, i] = sound
    for k, value in enumerate(slopes_of(temp, gamma, square, table_ref)):
        prim_ref[SLOPES + k, i] = value
    prim_ref[PRIMS, i] = pressure


def fill_split(u, i, normal, alpha, prim_ref, up_ref, down_ref):
    speed = prim_ref[VEL + normal, i]
    push = 0.5 * prim_ref[PRIMS, i]
    half = 0.5 * speed
    lean = 0.5 * alpha
    plus, minus = half + lean, half - lean
    for ref, factor in ((up_ref, plus), (down_ref, minus)):
        for k in range(NVAR):
            value = u[k] * factor
            if k == NS + normal:
                value = value + push
            if k == NS + 3:
                value = value + push * speed
            ref[k, i] = value
        ref[TOTAL, i] = tree(u[:NS]) * factor


def compute(
    nasa_ref, gas_ref, index_ref, kind_ref, speeds_ref, x_ref, hx_ref, hy_ref, out_ref,
    table_ref, prim_ref, up_ref, down_ref, dup_ref, ddown_ref,
    fx_ref, fz_ref, acc_ref, edge_ref,
):
    lanes = x_ref.shape[1]
    tile = (8, lanes)
    block = 64
    fill_table(nasa_ref, gas_ref, index_ref, table_ref)
    alphas = [speeds_ref[d] for d in range(3)]

    def own(r, x):
        return x_ref[pl.ds(pl.multiple_of(r * block + x * 8, 8), 8), :]

    def turned(r, y):
        return x_ref[pl.ds(r * block + y, 8, stride=8), :]

    def differences(count):
        def step(i, _):
            for k in range(NVAR + 1):
                dup_ref[k, i] = up_ref[k, i + 1] - up_ref[k, i]
                ddown_ref[k, i] = down_ref[k, i + 1] - down_ref[k, i]
            return 0

        lax.fori_loop(0, count, step, 0)

    def faces_across(normal, flux_ref):
        def step(i, _):
            def linear(r):
                here = up_ref[r, i + 2] + down_ref[r, i + 3]
                ahead = dup_ref[r, i + 2] - ddown_ref[r, i + 2]
                return 6.0 * here + (ahead + ahead) + (dup_ref[r, i + 1] - ddown_ref[r, i + 3])

            def put(r, value):
                flux_ref[r, i] = value

            face(
                normal,
                lambda r, k: dup_ref[r, i + k],
                lambda r, k: ddown_ref[r, i + 4 - k],
                lambda q: 0.5 * (prim_ref[q, i + 2] + prim_ref[q, i + 3]),
                linear,
                put,
            )
            return 0

        lax.fori_loop(0, 9, step, 0)

    def y_cells(i, read):
        u = read()
        fill_cells(u, i, table_ref, prim_ref)
        fill_split(u, i, 1, alphas[1], prim_ref, up_ref, down_ref)

    def y_own(y, _):
        y_cells(y + 3, lambda: [turned(r, y) for r in range(NVAR)])
        return 0

    def y_halo(k, _):
        y_cells(k, lambda: [hy_ref[0, r, k] for r in range(NVAR)])
        y_cells(k + 11, lambda: [hy_ref[1, r, k] for r in range(NVAR)])
        return 0

    def x_own(x, _):
        u = [own(r, x) for r in range(NVAR)]
        fill_cells(u, x + 3, table_ref, prim_ref)
        fill_split(u, x + 3, 0, alphas[0], prim_ref, up_ref, down_ref)
        return 0

    def x_halo(k, _):
        for side, base in ((0, 0), (1, 11)):
            u = [hx_ref[side, r, k] for r in range(NVAR)]
            fill_cells(u, k + base, table_ref, prim_ref)
            fill_split(u, k + base, 0, alphas[0], prim_ref, up_ref, down_ref)
        return 0

    lane = lax.broadcasted_iota(jnp.int32, tile, 1)

    width = 16
    spot = lane % width
    reach = spot - 3
    low_wall, high_wall = kind_ref[0] == 1, kind_ref[1] == 1
    low = jnp.where(reach < 0, jnp.where(low_wall, -1 - reach, 0), reach)
    beyond = spot - 13
    high = jnp.where(
        beyond >= 0,
        jnp.where(high_wall, lanes - 1 - beyond, lanes - 1),
        lanes + beyond,
    )
    source = jnp.where(spot < 8, low, high)
    mirrored = ((spot < 3) & low_wall) | ((spot > 12) & high_wall)
    sign = jnp.where(mirrored, -1.0, 1.0)
    group = lane // width

    def gather(values, index):
        return jnp.take_along_axis(values, index, axis=1)

    def z_edge(x, _):
        for r in range(NVAR):
            value = gather(own(r, x), source)
            if r == NS + 2:
                value = value * sign
            edge_ref[r] = jnp.where(group == x, value, edge_ref[r])
        return 0

    def roll(values, shift):
        return values if shift % lanes == 0 else pltpu.roll(values, shift % lanes, 1)

    def z_split(u, i):
        fill_split(u, i, 2, alphas[2], prim_ref, up_ref, down_ref)
        for k in range(NVAR + 1):
            dup_ref[k, i] = roll(up_ref[k, i], -1) - up_ref[k, i]
            ddown_ref[k, i] = roll(down_ref[k, i], -1) - down_ref[k, i]

    def z_own(x, _):
        u = [own(r, x) for r in range(NVAR)]
        z_split(u, x + 3)
        return 0

    def z_faces(x, _):
        i = x + 3

        def linear(r):
            here = up_ref[r, i] + roll(down_ref[r, i], -1)
            ahead = dup_ref[r, i] - ddown_ref[r, i]
            return 6.0 * here + (ahead + ahead) + (
                roll(dup_ref[r, i], 1) - roll(ddown_ref[r, i], -1)
            )

        def mean(q):
            value = prim_ref[q, i]
            return 0.5 * (value + roll(value, -1))

        def put(r, value):
            fz_ref[r, x] = value

        face(
            2,
            lambda r, k: roll(dup_ref[r, i], 2 - k),
            lambda r, k: roll(ddown_ref[r, i], k - 2),
            mean,
            linear,
            put,
        )
        return 0

    lax.fori_loop(0, 3, y_halo, 0)
    lax.fori_loop(0, 8, y_own, 0)
    differences(13)
    faces_across(1, fx_ref)

    def y_rate(y, _):
        for r in range(NVAR):
            acc_ref[pl.ds(r * block + y, 8, stride=8), :] = fx_ref[r, y + 1] - fx_ref[r, y]
        return 0

    lax.fori_loop(0, 8, y_rate, 0)

    lax.fori_loop(0, 3, x_halo, 0)
    lax.fori_loop(0, 8, x_own, 0)
    differences(13)
    faces_across(0, fx_ref)

    for r in range(NVAR):
        edge_ref[r] = jnp.zeros(tile, jnp.float32)
    lax.fori_loop(0, 8, z_edge, 0)
    edge = [edge_ref[r] for r in range(NVAR)]
    fill_cells(edge, 11, table_ref, prim_ref)
    z_split(edge, 11)
    lax.fori_loop(0, 8, z_own, 0)
    lax.fori_loop(0, 9, z_faces, 0)

    scale = (-COURANT / 6.0) / (alphas[0] + alphas[1] + alphas[2])
    near = jnp.where(lane < 2, lane + 3, lane - lanes + 13)
    patched = (lane < 2) | (lane > lanes - 4)

    def finish(x, _):
        first = jnp.clip(width * x + near, 0, lanes - 1)
        below = jnp.full(tile, width * x + 2, jnp.int32)
        for r in range(NVAR):
            edges = fz_ref[r, 8]
            upper = jnp.where(patched, gather(edges, first), fz_ref[r, x])
            lower = jnp.where(lane == 0, gather(edges, below), roll(upper, 1))
            rows = pl.ds(pl.multiple_of(r * block + x * 8, 8), 8)
            rate = (upper - lower) + (fx_ref[r, x + 1] - fx_ref[r, x]) + acc_ref[rows, :]
            out_ref[rows, :] = scale * rate
        return 0

    lax.fori_loop(0, 8, finish, 0)


def increment(nasa_table, gas_constant, species_index, kinds, speeds, flat, hx, hy):
    lanes = flat.shape[1]
    smem = pl.BlockSpec(memory_space=pltpu.SMEM)
    vmem = pl.BlockSpec(memory_space=pltpu.VMEM)

    def buffer(*shape):
        return pltpu.VMEM(shape + (8, lanes), jnp.float32)

    return pl.pallas_call(
        compute,
        out_shape=jax.ShapeDtypeStruct(flat.shape, jnp.float32),
        in_specs=[smem] * 4 + [vmem] * 4,
        out_specs=vmem,
        scratch_shapes=[
            buffer(TABLE),
            buffer(PRIMS + 1, 14),
            buffer(NVAR + 1, 14),
            buffer(NVAR + 1, 14),
            buffer(NVAR + 1, 14),
            buffer(NVAR + 1, 14),
            buffer(NVAR, 9),
            buffer(NVAR, 9),
            pltpu.VMEM(flat.shape, jnp.float32),
            buffer(NVAR),
        ],
        name="increment",
    )(nasa_table, gas_constant, species_index, kinds, speeds, flat, hx, hy)


def speed_kernel(nasa_ref, gas_ref, index_ref, x_ref, out_ref, table_ref):
    block = 64
    fill_table(nasa_ref, gas_ref, index_ref, table_ref)

    def step(x, best):
        u = [x_ref[pl.ds(pl.multiple_of(r * block + x * 8, 8), 8), :] for r in range(NVAR)]
        _, vel, _, _, _, _, sound = thermo(u, table_ref)
        return tuple(jnp.maximum(b, jnp.abs(v) + sound) for b, v in zip(best, vel))

    zero = jnp.zeros((8, x_ref.shape[1]), jnp.float32)
    for d, value in enumerate(lax.fori_loop(0, 8, step, (zero, zero, zero))):
        out_ref[d] = value


def shards(preserved_vector, nasa_table, gas_constant, species_index, face_kind):
    _, nx, ny, lanes = preserved_vector.shape
    flat = preserved_vector.reshape(NVAR * nx * ny, lanes)
    smem = pl.BlockSpec(memory_space=pltpu.SMEM)
    vmem = pl.BlockSpec(memory_space=pltpu.VMEM)
    local = pl.pallas_call(
        speed_kernel,
        out_shape=jax.ShapeDtypeStruct((3, 8, lanes), jnp.float32),
        in_specs=[smem] * 3 + [vmem],
        out_specs=vmem,
        scratch_shapes=[pltpu.VMEM((TABLE, 8, lanes), jnp.float32)],
        name="speeds",
    )(nasa_table, gas_constant, species_index, flat)
    speeds = lax.pmax(jnp.max(local, axis=(1, 2)), ("gx", "gy"))
    speeds = jnp.broadcast_to(speeds[:, None, None], (3, 8, lanes))

    def swap(low, high, axis):
        n = lax.axis_size(axis)
        ahead = [(i, (i + 1) % n) for i in range(n)]
        back = [(b, a) for a, b in ahead]
        return jnp.stack([lax.ppermute(high, axis, ahead), lax.ppermute(low, axis, back)])

    hx = swap(preserved_vector[:, :3], preserved_vector[:, -3:], "gx")
    turned = jnp.swapaxes(preserved_vector, 1, 2)
    hy = swap(turned[:, :3], turned[:, -3:], "gy")
    out = increment(
        nasa_table, gas_constant, species_index, face_kind.reshape(2), speeds, flat, hx, hy
    )
    return out.reshape(preserved_vector.shape)


def solution(mesh):
    return jax.shard_map(
        shards,
        mesh=mesh,
        in_specs=(P(None, "gx", "gy", None), P(), P(), P(), P("gx", "gy", None)),
        out_specs=P(None, "gx", "gy", None),
        check_vma=False,
    )
```

time: 108 us -> 69.4 us (0.64)
  other arithmetic: 35.4 us -> 2.32 us
  Pallas kernels: 0 us -> 18.3 us
  local copies, waits for them, and re-layouts: 19.5 us -> 2.51 us
  between operations: 2.88 us -> 0.03 us
  blocking collectives: 40.2 us -> 37.8 us
  matrix products: 1.7 us -> 0 us
    pallas_call x0 -> x2, Pallas kernels: none -> 18.3 us  [the longest x1 16 us: increment(): pl.pallas_call(compute, out_shape=jax.ShapeDtypeStruct(flat.shape, jnp.fl...]
    add x5 -> x0, other arithmetic: 10.8 us -> none  [the longest x3 9.05 us: direction_rate(): amplitude = rising + falling]
    slice x10 -> x2, local copies, waits for them, and re-layouts: 9.41 us -> 0.05 us  [the longest x1 0.02 us: shards(): hy = swap(turned[:, :3], turned[:, -3:], 'gy')]
    unnamed x57 -> x0, other arithmetic: 6.56 us -> none
    mul x21 -> x0, other arithmetic: 6.03 us -> none  [the longest x3 3.87 us: direction_rate(): downwind = 0.5 * (physical - speed * preserved_vector_lines)]
    reduce_sum x17 -> x0, other arithmetic: 5.89 us -> none  [the longest x2 1.43 us: solve_for_kelvin(): jnp.sum(prefix_addition_result * blend_stack_lane * (chemical_heat_conten...]
    unnamed x24 -> x6, local copies, waits for them, and re-layouts: 5.37 us -> 1.79 us
    rev x2 -> x0, local copies, waits for them, and re-layouts: 3.4 us -> none  [the longest x1 2.18 us: wall_pad(): lower_mirror = payload[..., 2::-1] * sign_flips]
  transfers between devices with their start and end apart: 4 -> 4, of which waited for: 0 -> 0; matrix products, arithmetic and copies ran while one was open for 34% -> 3% of each run, Pallas kernels for 0% -> 3%
where the time goes in v1:
time: 69.4 us; the launch traced here: 69 us
  blocking collectives  37.8 us (54%)
  Pallas kernels  18.3 us (26%)
  starting transfers between devices  7.95 us (11%)
  local copies, waits for them, and re-layouts  2.51 us (4%)
  other arithmetic  2.32 us (3%)
    pmax x1, blocking collectives, shards(): speeds = lax.pmax(jnp.max(local, axis=(1, 2)), ('gx', 'gy'))  37.8 us
    pallas_call x1, Pallas kernels, increment(): pl.pallas_call(compute, out_shape=jax.ShapeDtypeStruct(flat.shape, jnp.fl...  16 us
    ppermute x2, starting transfers between devices, swap(): lax.ppermute(low, axis, back)  5.08 us
    ppermute x2, starting transfers between devices, swap(): lax.ppermute(high, axis, ahead)  2.87 us
    pallas_call x1, Pallas kernels, shards(): pl.pallas_call(speed_kernel, out_shape=jax.ShapeDtypeStruct((3, 8, lanes)...  2.34 us
    unnamed x6, local copies, waits for them, and re-layouts  1.79 us
    another operation x2, other arithmetic, swap(): jnp.stack([lax.ppermute(high, axis, ahead), lax.ppermute(low, axis, back)])  1.51 us
  transfers between devices with their start and end apart: 4, of which 0 were waited for; matrix products, arithmetic and copies ran while one was open for 3% of the time, Pallas kernels for 3%

profile of v1, /device:TPU:0, one launch (start us, length us, event | category | flops | bytes accessed | tf_op | source)
XLA Modules:
  0.0 69.0 jit_solution(9655390467606136898)
XLA Ops:
  0.0 1.1 %copy.10 = f32[14,8,8,128]{3,1,2,0:T(8,128)S(1)} copy(f32[14,8,8,128]{3,2,1,0:T(8,128)} %param.5) | data formatting | bytes 917504 | tf_op args[0]
  1.1 0.0 copy-start
  1.1 0.5 collective-permute-start.2
  1.7 2.0 %collective-permute-start.3 = (f32[14,3,8,128]{3,2,1,0:T(8,128)S(1)}, f32[14,3,8,128]{3,2,1,0:T(8,128)S(1)}, u32[]{:S(2)}, u32[]{:S(2)}) collective-permute-start(f32[14,3,8,128]{3,2,1,0:T(8,128)S(1)} %get-tuple-element.6), channel_id=1, source_target_pairs={{1,0},{2,1},{3,2},{0,3},{5,4},{6,5},{7,6},{4,7},{9,8},{10,9},{11,1... | collective-permute-start | bytes 516104 | tf_op jit(solution)/shard_map/ppermute | solution.py:449
  3.7 0.0 copy-done
  3.7 0.0 copy-start.1
  3.7 2.3 %collective-permute-start = (f32[14,3,8,128]{3,2,1,0:T(8,128)S(1)}, f32[14,3,8,128]{3,2,1,0:T(8,128)S(1)}, u32[]{:S(2)}, u32[]{:S(2)}) collective-permute-start(f32[14,3,8,128]{3,2,1,0:T(8,128)S(1)} %get-tuple-element.7), channel_id=1, source_target_pairs={{0,4},{4,8},{8,12},{12,16},{16,20},{20,24},{24,28},{28,0},{1,5},{5... | collective-permute-start | bytes 516104 | tf_op jit(solution)/shard_map/ppermute | solution.py:449
  6.0 3.1 %collective-permute-start.1 = (f32[14,3,8,128]{3,2,1,0:T(8,128)S(1)}, f32[14,3,8,128]{3,2,1,0:T(8,128)S(1)}, u32[]{:S(2)}, u32[]{:S(2)}) collective-permute-start(f32[14,3,8,128]{3,2,1,0:T(8,128)S(1)} %get-tuple-element.8), channel_id=1, source_target_pairs={{4,0},{8,4},{12,8},{16,12},{20,16},{24,20},{28,24},{0,28},{5,1},{9... | collective-permute-start | bytes 516104 | tf_op jit(solution)/shard_map/ppermute | solution.py:449
  9.1 0.0 copy-done.1
  9.1 0.7 copy.8.nasa_ref
  9.8 2.3 %speeds.1 = f32[3,8,128]{2,1,0:T(8,128)} custom-call(f32[32,6]{1,0:T(8,128)} %copy.8.nasa_ref, f32[32]{0:T(128)} %gas_ref.3, s32[9]{0:T(128)} %index_ref.3, f32[896,128]{1,0:T(8,128)} %bitcast.10), custom_call_target="tpu_custom_call" | custom-call | tf_op jit(solution)/shard_map/speeds/pallas_call | solution.py:434
  12.2 0.8 %reduce_max.9 = f32[3]{0:T(128)S(1)} reduce(f32[3,8,128]{2,1,0:T(8,128)} %speeds.1, f32[]{:T(128)} %constant.0.clone.1), dimensions={1,2}, to_apply=%region_0.0 | reduce | flops 3069 | bytes 12304 | tf_op jit(solution)/shard_map/reduce_max | solution.py:442
  13.0 37.8 %pmax.7 = f32[3]{0:T(128)S(1)} all-reduce(f32[3]{0:T(128)S(1)} %reduce_max.9), channel_id=1, replica_groups=mesh['gx'=8,'gy'=4] {'gx','gy'}, use_global_device_ids=true, to_apply=%region_1.0 | all-reduce | flops 3 | bytes 24 | tf_op jit(solution)/shard_map/pmax | solution.py:442
  50.8 0.0 collective-permute-done.2
  50.8 0.0 collective-permute-done.3
  50.8 0.8 %pad_maximum_fusion.1.hy_ref = f32[2,14,3,8,128]{4,3,2,1,0:T(8,128)} fusion(f32[1,14,3,8,128]{4,3,2,1,0:T(8,128)S(1)} %bitcast.15, f32[1,14,3,8,128]{4,3,2,1,0:T(8,128)S(1)} %bitcast.13), kind=kLoop, calls=%fused_computation.2 | loop fusion | flops 86016 | bytes 688128 | tf_op jit(solution)/shard_map/stack | solution.py:449
  51.6 0.0 collective-permute-done
  51.6 0.0 collective-permute-done.1
  51.6 0.7 %pad_maximum_fusion.hx_ref = f32[2,14,3,8,128]{4,3,2,1,0:T(8,128)} fusion(f32[1,14,3,8,128]{4,3,2,1,0:T(8,128)S(1)} %bitcast.16, f32[1,14,3,8,128]{4,3,2,1,0:T(8,128)S(1)} %bitcast.14), kind=kLoop, calls=%fused_computation.1 | loop fusion | flops 86016 | bytes 688128 | tf_op jit(solution)/shard_map/stack | solution.py:449
  52.3 0.7 broadcast_in_dim.2.speeds_ref
  53.0 16.0 %increment.1 = f32[896,128]{1,0:T(8,128)} custom-call(f32[32,6]{1,0:T(8,128)} %copy.8.nasa_ref, f32[32]{0:T(128)} %gas_ref.3, s32[9]{0:T(128)} %index_ref.3, s32[2]{0:T(128)} %bitcast.17, f32[3,8,128]{2,1,0:T(8,128)} %broadcast_in_dim.2.speeds_ref, f32[896,128]{1,0:T(8,128)} %bitcast.11, f32[2,14,3,8,128]{4,3,2,1,0:T(8,128)} %pad_maximum_fusion.hx_ref, ...), custom_call_target="tpu_custom_call" | custom-call | tf_op jit(solution)/shard_map/increment/pallas_call | solution.py:394
  (2 shorter events, 0.0 us)
Async XLA Ops:
  1.1 2.6 %copy-start = (f32[14,8,8,128]{3,2,1,0:T(8,128)S(1)}, f32[14,8,8,128]{3,2,1,0:T(8,128)}, u32[]{:S(2)}) copy-start(f32[14,8,8,128]{3,2,1,0:T(8,128)} %param.5) | copy-start | bytes 1376260
  1.1 49.7 %collective-permute-start.2 = (f32[14,3,8,128]{3,2,1,0:T(8,128)S(1)}, f32[14,3,8,128]{3,2,1,0:T(8,128)S(1)}, u32[]{:S(2)}, u32[]{:S(2)}) collective-permute-start(f32[14,3,8,128]{3,2,1,0:T(8,128)S(1)} %get-tuple-element.5), channel_id=1, source_target_pairs={{0,1},{1,2},{2,3},{3,0},{4,5},{5,6},{6,7},{7,4},{8,9},{9,10},{10,1... | collective-permute-start | bytes 516104 | tf_op jit(solution)/shard_map/ppermute | solution.py:449
  1.7 49.1 %collective-permute-start.3 = (f32[14,3,8,128]{3,2,1,0:T(8,128)S(1)}, f32[14,3,8,128]{3,2,1,0:T(8,128)S(1)}, u32[]{:S(2)}, u32[]{:S(2)}) collective-permute-start(f32[14,3,8,128]{3,2,1,0:T(8,128)S(1)} %get-tuple-element.6), channel_id=1, source_target_pairs={{1,0},{2,1},{3,2},{0,3},{5,4},{6,5},{7,6},{4,7},{9,8},{10,9},{11,1... | collective-permute-start | bytes 516104 | tf_op jit(solution)/shard_map/ppermute | solution.py:449
  3.7 5.5 %copy-start.1 = (f32[32,6]{0,1:T(8,128)S(1)}, f32[32,6]{0,1:T(8,128)}, u32[]{:S(2)}) copy-start(f32[32,6]{0,1:T(8,128)} %param.6) | copy-start | bytes 2308
  3.7 47.9 %collective-permute-start = (f32[14,3,8,128]{3,2,1,0:T(8,128)S(1)}, f32[14,3,8,128]{3,2,1,0:T(8,128)S(1)}, u32[]{:S(2)}, u32[]{:S(2)}) collective-permute-start(f32[14,3,8,128]{3,2,1,0:T(8,128)S(1)} %get-tuple-element.7), channel_id=1, source_target_pairs={{0,4},{4,8},{8,12},{12,16},{16,20},{20,24},{24,28},{28,0},{1,5},{5... | collective-permute-start | bytes 516104 | tf_op jit(solution)/shard_map/ppermute | solution.py:449
  6.0 45.6 %collective-permute-start.1 = (f32[14,3,8,128]{3,2,1,0:T(8,128)S(1)}, f32[14,3,8,128]{3,2,1,0:T(8,128)S(1)}, u32[]{:S(2)}, u32[]{:S(2)}) collective-permute-start(f32[14,3,8,128]{3,2,1,0:T(8,128)S(1)} %get-tuple-element.8), channel_id=1, source_target_pairs={{4,0},{8,4},{12,8},{16,12},{20,16},{24,20},{28,24},{0,28},{5,1},{9... | collective-permute-start | bytes 516104 | tf_op jit(solution)/shard_map/ppermute | solution.py:449

commit v2 on v1

--- a/solution.py
+++ b/solution.py
@@ -23,12 +23,12 @@
         gas = gas_ref[row]
         values = [
             gas,
-            gas * nasa_ref[row, 5],
-            gas * (nasa_ref[row, 0] - 1.0),
-            gas * nasa_ref[row, 1] * (1.0 / 2.0),
-            gas * nasa_ref[row, 2] * (1.0 / 3.0),
-            gas * nasa_ref[row, 3] * (1.0 / 4.0),
-            gas * nasa_ref[row, 4] * (1.0 / 5.0),
+            gas * nasa_ref[5, row],
+            gas * (nasa_ref[0, row] - 1.0),
+            gas * nasa_ref[1, row] * (1.0 / 2.0),
+            gas * nasa_ref[2, row] * (1.0 / 3.0),
+            gas * nasa_ref[3, row] * (1.0 / 4.0),
+            gas * nasa_ref[4, row] * (1.0 / 5.0),
         ]
         for n, value in enumerate(values):
             table_ref[n * NS + i] = jnp.full(table_ref.shape[1:], value, jnp.float32)
@@ -251,8 +251,12 @@
         return 0
 
     def y_halo(k, _):
-        y_cells(k, lambda: [hy_ref[0, r, k] for r in range(NVAR)])
-        y_cells(k + 11, lambda: [hy_ref[1, r, k] for r in range(NVAR)])
+        for side, base in ((0, 0), (1, 11)):
+            first = side * NVAR * 24 + k
+            y_cells(
+                k + base,
+                lambda: [hy_ref[pl.ds(first + r * 24, 8, stride=3), :] for r in range(NVAR)],
+            )
         return 0
 
     def x_own(x, _):
@@ -412,47 +416,132 @@
     )(nasa_table, gas_constant, species_index, kinds, speeds, flat, hx, hy)
 
 
-def speed_kernel(nasa_ref, gas_ref, index_ref, x_ref, out_ref, table_ref):
-    block = 64
+MESH = pl.DeviceIdType.MESH
+
+
+def exchange(
+    size_x, size_y,
+    nasa_ref, gas_ref, index_ref, x_ref, source_ref,
+    speeds_ref, hx_ref, hy_ref,
+    table_ref, mine_ref, line_ref, slots_y, slots_x,
+    small_send, recv_y, recv_x, big_send, big_recv,
+):
+    gx, gy = lax.axis_index("gx"), lax.axis_index("gy")
+    nx, ny = source_ref.shape[1], source_ref.shape[2]
+
+    def along_x(offset):
+        return (lax.rem(gx + offset, size_x), gy)
+
+    def along_y(offset):
+        return (gx, lax.rem(gy + offset, size_y))
+
+    barrier = pltpu.get_barrier_semaphore()
+    for n, along in ((size_x, along_x), (size_y, along_y)):
+        for offset in range(1, n):
+            pl.semaphore_signal(barrier, inc=1, device_id=along(offset), device_id_type=MESH)
+    pl.semaphore_wait(barrier, size_x + size_y - 2)
+
+    halos = []
+    for n, (source, target, device) in enumerate(
+        (
+            (source_ref.at[:, pl.ds(nx - 3, 3)], hx_ref.at[0], along_x(1)),
+            (source_ref.at[:, pl.ds(0, 3)], hx_ref.at[1], along_x(size_x - 1)),
+            (source_ref.at[:, :, pl.ds(ny - 3, 3)], hy_ref.at[0], along_y(1)),
+            (source_ref.at[:, :, pl.ds(0, 3)], hy_ref.at[1], along_y(size_y - 1)),
+        )
+    ):
+        copy = pltpu.make_async_remote_copy(
+            src_ref=source,
+            dst_ref=target,
+            send_sem=big_send.at[n],
+            recv_sem=big_recv.at[n],
+            device_id=device,
+            device_id_type=MESH,
+        )
+        copy.start()
+        halos.append(copy)
+
     fill_table(nasa_ref, gas_ref, index_ref, table_ref)
+    block = nx * ny
 
     def step(x, best):
         u = [x_ref[pl.ds(pl.multiple_of(r * block + x * 8, 8), 8), :] for r in range(NVAR)]
         _, vel, _, _, _, _, sound = thermo(u, table_ref)
         return tuple(jnp.maximum(b, jnp.abs(v) + sound) for b, v in zip(best, vel))
 
-    zero = jnp.zeros((8, x_ref.shape[1]), jnp.float32)
-    for d, value in enumerate(lax.fori_loop(0, 8, step, (zero, zero, zero))):
-        out_ref[d] = value
+    tile = mine_ref.shape
+    zero = jnp.zeros(tile, jnp.float32)
+    best = lax.fori_loop(0, nx, step, (zero, zero, zero))
+    best = [jnp.max(b, axis=(0, 1), keepdims=True) for b in best]
+    row = lax.broadcasted_iota(jnp.int32, tile, 0)
+    value = jnp.where(row == 0, best[0], jnp.where(row == 1, best[1], best[2]))
+
+    for n, along, held, slots, recv, base in (
+        (size_y, along_y, mine_ref, slots_y, recv_y, 0),
+        (size_x, along_x, line_ref, slots_x, recv_x, size_y),
+    ):
+        held[...] = value
+        copies = []
+        for offset in range(1, n):
+            copy = pltpu.make_async_remote_copy(
+                src_ref=held,
+                dst_ref=slots.at[offset],
+                send_sem=small_send.at[base + offset],
+                recv_sem=recv.at[offset],
+                device_id=along(offset),
+                device_id_type=MESH,
+            )
+            copy.start()
+            copies.append(copy)
+        for offset, copy in enumerate(copies, 1):
+            copy.wait()
+            value = jnp.maximum(value, slots[offset])
+    for d in range(3):
+        speeds_ref[d] = jnp.broadcast_to(value[d : d + 1], tile)
+    for copy in halos:
+        copy.wait()
 
 
 def shards(preserved_vector, nasa_table, gas_constant, species_index, face_kind):
     _, nx, ny, lanes = preserved_vector.shape
+    size_x, size_y = lax.axis_size("gx"), lax.axis_size("gy")
     flat = preserved_vector.reshape(NVAR * nx * ny, lanes)
+    nasa_table = nasa_table.T
     smem = pl.BlockSpec(memory_space=pltpu.SMEM)
     vmem = pl.BlockSpec(memory_space=pltpu.VMEM)
-    local = pl.pallas_call(
-        speed_kernel,
-        out_shape=jax.ShapeDtypeStruct((3, 8, lanes), jnp.float32),
-        in_specs=[smem] * 3 + [vmem],
-        out_specs=vmem,
-        scratch_shapes=[pltpu.VMEM((TABLE, 8, lanes), jnp.float32)],
-        name="speeds",
-    )(nasa_table, gas_constant, species_index, flat)
-    speeds = lax.pmax(jnp.max(local, axis=(1, 2)), ("gx", "gy"))
-    speeds = jnp.broadcast_to(speeds[:, None, None], (3, 8, lanes))
-
-    def swap(low, high, axis):
-        n = lax.axis_size(axis)
-        ahead = [(i, (i + 1) % n) for i in range(n)]
-        back = [(b, a) for a, b in ahead]
-        return jnp.stack([lax.ppermute(high, axis, ahead), lax.ppermute(low, axis, back)])
-
-    hx = swap(preserved_vector[:, :3], preserved_vector[:, -3:], "gx")
-    turned = jnp.swapaxes(preserved_vector, 1, 2)
-    hy = swap(turned[:, :3], turned[:, -3:], "gy")
+    anywhere = pl.BlockSpec(memory_space=pl.ANY)
+    shape = functools.partial(jax.ShapeDtypeStruct, dtype=jnp.float32)
+    dma = pltpu.SemaphoreType.DMA
+    speeds, hx, hy = pl.pallas_call(
+        functools.partial(exchange, size_x, size_y),
+        out_shape=(
+            shape((3, 8, lanes)),
+            shape((2, NVAR, 3, ny, 1, lanes)),
+            shape((2, NVAR, nx, 3, 1, lanes)),
+        ),
+        in_specs=[smem] * 3 + [vmem, anywhere],
+        out_specs=(vmem, anywhere, anywhere),
+        scratch_shapes=[
+            pltpu.VMEM((TABLE, 8, lanes), jnp.float32),
+            pltpu.VMEM((8, lanes), jnp.float32),
+            pltpu.VMEM((8, lanes), jnp.float32),
+            pltpu.VMEM((size_y, 8, lanes), jnp.float32),
+            pltpu.VMEM((size_x, 8, lanes), jnp.float32),
+            dma((size_x + size_y,)),
+            dma((size_y,)),
+            dma((size_x,)),
+            dma((4,)),
+            dma((4,)),
+        ],
+        compiler_params=pltpu.CompilerParams(collective_id=0, has_side_effects=True),
+        name="exchange",
+    )(
+        nasa_table, gas_constant, species_index, flat,
+        preserved_vector.reshape(NVAR, nx, ny, 1, lanes),
+    )
     out = increment(
-        nasa_table, gas_constant, species_index, face_kind.reshape(2), speeds, flat, hx, hy
+        nasa_table, gas_constant, species_index, face_kind.reshape(2), speeds, flat,
+        hx.reshape(2, NVAR, 3, ny, lanes), hy.reshape(2 * NVAR * nx * 3, lanes),
     )
     return out.reshape(preserved_vector.shape)
 

time: 69.4 us -> 33.1 us (0.48)
  blocking collectives: 37.8 us -> 0 us
  Pallas kernels: 18.3 us -> 32.9 us
  starting transfers between devices: 7.95 us -> 0 us
  local copies, waits for them, and re-layouts: 2.51 us -> 0 us
  other arithmetic: 2.32 us -> 0 us
    pmax x1 -> x0, blocking collectives: 37.8 us -> none  [shards(): speeds = lax.pmax(jnp.max(local, axis=(1, 2)), ('gx', 'gy'))]
    pallas_call x1, Pallas kernels: 2.34 us -> 17 us  [shards(): pl.pallas_call(functools.partial(exchange, size_x, size_y), out_shape=(sh...]
    ppermute x4 -> x0, starting transfers between devices: 7.95 us -> none  [the longest x2 5.08 us: swap(): lax.ppermute(low, axis, back)]
    unnamed x6 -> x0, local copies, waits for them, and re-layouts: 1.79 us -> none
    another operation x2 -> x0, other arithmetic: 1.51 us -> none  [swap(): jnp.stack([lax.ppermute(high, axis, ahead), lax.ppermute(low, axis, back)])]
    reduce_max x1 -> x0, other arithmetic: 0.81 us -> none  [shards(): speeds = lax.pmax(jnp.max(local, axis=(1, 2)), ('gx', 'gy'))]
  transfers between devices with their start and end apart: 4 -> 0, of which waited for: 0 -> 0; matrix products, arithmetic and copies ran while one was open for 3% -> 0% of each run, Pallas kernels for 3% -> 0%
where the time goes in v2:
time: 33.1 us; the launch traced here: 32.9 us
  Pallas kernels  32.9 us (99%)
    pallas_call x1, Pallas kernels, shards(): pl.pallas_call(functools.partial(exchange, size_x, size_y), out_shape=(sh...  17 us
    pallas_call x1, Pallas kernels, increment(): pl.pallas_call(compute, out_shape=jax.ShapeDtypeStruct(flat.shape, jnp.fl...  16 us

profile of v2, /device:TPU:0, one launch (start us, length us, event | category | flops | bytes accessed | tf_op | source)
XLA Modules:
  0.0 32.9 jit_solution(10078873604929962061)
XLA Ops:
  0.0 17.0 %exchange.1 = (f32[3,8,128]{2,1,0:T(8,128)}, f32[2,14,3,8,1,128]{5,4,3,2,1,0:T(1,128)}, f32[2,14,8,3,1,128]{5,4,3,2,1,0:T(1,128)}) custom-call(f32[6,32]{1,0:T(8,128)} %bitcast.12, f32[32]{0:T(128)} %gas_ref.3, s32[9]{0:T(128)} %index_ref.3, f32[896,128]{1,0:T(8,128)} %bitcast.7, f32[14,8,8,1,128]{4,3,2,1,0:T(1,128)} %bitcast.8), custom_call_target="tpu_custom_call" | custom-call | tf_op jit(solution)/shard_map/exchange/pallas_call | solution.py:515
  17.0 16.0 %increment.1 = f32[896,128]{1,0:T(8,128)} custom-call(f32[6,32]{1,0:T(8,128)} %bitcast.13, f32[32]{0:T(128)} %gas_ref.3, s32[9]{0:T(128)} %index_ref.3, s32[2]{0:T(128)} %bitcast.14, f32[3,8,128]{2,1,0:T(8,128)} %get-tuple-element.8.speeds_ref, f32[896,128]{1,0:T(8,128)} %bitcast.9, f32[2,14,3,8,128]{4,3,2,1,0:T(8,128)} %bitcast.10, f32[672,128]{1,0:T(8,128)} %bitcast.11), custom_call_target="tpu_custom_call" | custom-call | tf_op jit(solution)/shard_map/increment/pallas_call | solution.py:398

commit v3 on v1

--- a/solution.py
+++ b/solution.py
@@ -23,12 +23,12 @@
         gas = gas_ref[row]
         values = [
             gas,
-            gas * nasa_ref[row, 5],
-            gas * (nasa_ref[row, 0] - 1.0),
-            gas * nasa_ref[row, 1] * (1.0 / 2.0),
-            gas * nasa_ref[row, 2] * (1.0 / 3.0),
-            gas * nasa_ref[row, 3] * (1.0 / 4.0),
-            gas * nasa_ref[row, 4] * (1.0 / 5.0),
+            gas * nasa_ref[5, row],
+            gas * (nasa_ref[0, row] - 1.0),
+            gas * nasa_ref[1, row] * (1.0 / 2.0),
+            gas * nasa_ref[2, row] * (1.0 / 3.0),
+            gas * nasa_ref[3, row] * (1.0 / 4.0),
+            gas * nasa_ref[4, row] * (1.0 / 5.0),
         ]
         for n, value in enumerate(values):
             table_ref[n * NS + i] = jnp.full(table_ref.shape[1:], value, jnp.float32)
@@ -193,16 +193,59 @@
         ref[TOTAL, i] = tree(u[:NS]) * factor
 
 
-def compute(
-    nasa_ref, gas_ref, index_ref, kind_ref, speeds_ref, x_ref, hx_ref, hy_ref, out_ref,
-    table_ref, prim_ref, up_ref, down_ref, dup_ref, ddown_ref,
+MESH = pl.DeviceIdType.MESH
+
+
+def fused(
+    size_x, size_y,
+    nasa_ref, gas_ref, index_ref, kind_ref, flat_ref, planes_ref, source_ref, out_ref,
+    x_ref, hx_ref, hy_ref, mine_ref, line_ref, slots_y, slots_x,
+    table_ref, prim_ref, turn_ref, up_ref, down_ref, dup_ref, ddown_ref,
     fx_ref, fz_ref, acc_ref, edge_ref,
+    load_sem, small_send, recv_y, recv_x, big_send, big_recv,
 ):
+    load = pltpu.make_async_copy(flat_ref, x_ref, load_sem)
+    load.start()
+    gx, gy = lax.axis_index("gx"), lax.axis_index("gy")
+    nx, ny = planes_ref.shape[1], planes_ref.shape[2]
+
+    def along_x(offset):
+        return (lax.rem(gx + offset, size_x), gy)
+
+    def along_y(offset):
+        return (gx, lax.rem(gy + offset, size_y))
+
+    barrier = pltpu.get_barrier_semaphore()
+    for n, along in ((size_x, along_x), (size_y, along_y)):
+        for offset in range(1, n):
+            pl.semaphore_signal(barrier, inc=1, device_id=along(offset), device_id_type=MESH)
+    fill_table(nasa_ref, gas_ref, index_ref, table_ref)
+    pl.semaphore_wait(barrier, size_x + size_y - 2)
+
+    halos = []
+    for n, (source, target, device) in enumerate(
+        (
+            (planes_ref.at[:, pl.ds(nx - 3, 3)], hx_ref.at[0], along_x(1)),
+            (planes_ref.at[:, pl.ds(0, 3)], hx_ref.at[1], along_x(size_x - 1)),
+            (source_ref.at[:, :, pl.ds(ny - 3, 3)], hy_ref.at[0], along_y(1)),
+            (source_ref.at[:, :, pl.ds(0, 3)], hy_ref.at[1], along_y(size_y - 1)),
+        )
+    ):
+        copy = pltpu.make_async_remote_copy(
+            src_ref=source,
+            dst_ref=target,
+            send_sem=big_send.at[n],
+            recv_sem=big_recv.at[n],
+            device_id=device,
+            device_id_type=MESH,
+        )
+        copy.start()
+        halos.append(copy)
+    load.wait()
+
     lanes = x_ref.shape[1]
     tile = (8, lanes)
-    block = 64
-    fill_table(nasa_ref, gas_ref, index_ref, table_ref)
-    alphas = [speeds_ref[d] for d in range(3)]
+    block = nx * ny
 
     def own(r, x):
         return x_ref[pl.ds(pl.multiple_of(r * block + x * 8, 8), 8), :]
@@ -219,7 +262,7 @@
 
         lax.fori_loop(0, count, step, 0)
 
-    def faces_across(normal, flux_ref):
+    def faces_across(normal, prim_ref, flux_ref):
         def step(i, _):
             def linear(r):
                 here = up_ref[r, i + 2] + down_ref[r, i + 3]
@@ -241,31 +284,29 @@
 
         lax.fori_loop(0, 9, step, 0)
 
-    def y_cells(i, read):
-        u = read()
-        fill_cells(u, i, table_ref, prim_ref)
-        fill_split(u, i, 1, alphas[1], prim_ref, up_ref, down_ref)
-
-    def y_own(y, _):
-        y_cells(y + 3, lambda: [turned(r, y) for r in range(NVAR)])
-        return 0
-
-    def y_halo(k, _):
-        y_cells(k, lambda: [hy_ref[0, r, k] for r in range(NVAR)])
-        y_cells(k + 11, lambda: [hy_ref[1, r, k] for r in range(NVAR)])
-        return 0
-
-    def x_own(x, _):
-        u = [own(r, x) for r in range(NVAR)]
-        fill_cells(u, x + 3, table_ref, prim_ref)
-        fill_split(u, x + 3, 0, alphas[0], prim_ref, up_ref, down_ref)
-        return 0
-
-    def x_halo(k, _):
-        for side, base in ((0, 0), (1, 11)):
-            u = [hx_ref[side, r, k] for r in range(NVAR)]
-            fill_cells(u, k + base, table_ref, prim_ref)
-            fill_split(u, k + base, 0, alphas[0], prim_ref, up_ref, down_ref)
+    def y_halo_tile(side, r, k):
+        return hy_ref[side, r, :, k, 0, :]
+
+    def cells_halo(normal, prims, read):
+        def step(k, _):
+            for side, base in ((0, 0), (1, 11)):
+                u = [read(side, r, k) for r in range(NVAR)]
+                fill_cells(u, k + base, table_ref, prims)
+                fill_split(u, k + base, normal, alphas[normal], prims, up_ref, down_ref)
+            return 0
+
+        lax.fori_loop(0, 3, step, 0)
+
+    def split_own(normal, prims, read):
+        def step(n, _):
+            u = [read(r, n) for r in range(NVAR)]
+            fill_split(u, n + 3, normal, alphas[normal], prims, up_ref, down_ref)
+            return 0
+
+        lax.fori_loop(0, 8, step, 0)
+
+    def y_prims(y, _):
+        fill_cells([turned(r, y) for r in range(NVAR)], y + 3, table_ref, turn_ref)
         return 0
 
     lane = lax.broadcasted_iota(jnp.int32, tile, 1)
@@ -312,7 +353,7 @@
         return 0
 
     def z_faces(x, _):
-        i = x + 3
+        i = jnp.where(x == 8, 14, x + 3)
 
         def linear(r):
             here = up_ref[r, i] + roll(down_ref[r, i], -1)
@@ -338,10 +379,62 @@
         )
         return 0
 
-    lax.fori_loop(0, 3, y_halo, 0)
-    lax.fori_loop(0, 8, y_own, 0)
+    def x_prims(x, best):
+        u = [own(r, x) for r in range(NVAR)]
+        fill_cells(u, x + 3, table_ref, prim_ref)
+        sound = prim_ref[SOUND, x + 3]
+        return tuple(
+            jnp.maximum(b, jnp.abs(prim_ref[VEL + d, x + 3]) + sound) for d, b in enumerate(best)
+        )
+
+    zero = jnp.zeros(tile, jnp.float32)
+    best = lax.fori_loop(0, 8, x_prims, (zero, zero, zero))
+    best = [jnp.max(b, axis=(0, 1), keepdims=True) for b in best]
+    row = lax.broadcasted_iota(jnp.int32, tile, 0)
+    value = jnp.where(row == 0, best[0], jnp.where(row == 1, best[1], best[2]))
+
+    def fill_turned():
+        lax.fori_loop(0, 8, y_prims, 0)
+
+    def fill_edge():
+        for r in range(NVAR):
+            edge_ref[r] = zero
+        lax.fori_loop(0, 8, z_edge, 0)
+        fill_cells([edge_ref[r] for r in range(NVAR)], 14, table_ref, prim_ref)
+
+    for n, along, held, slots, recv, base, meanwhile in (
+        (size_y, along_y, mine_ref, slots_y, recv_y, 0, fill_edge),
+        (size_x, along_x, line_ref, slots_x, recv_x, size_y, fill_turned),
+    ):
+        held[...] = value
+        copies = []
+        for offset in range(1, n):
+            copy = pltpu.make_async_remote_copy(
+                src_ref=held,
+                dst_ref=slots.at[offset],
+                send_sem=small_send.at[base + offset],
+                recv_sem=recv.at[offset],
+                device_id=along(offset),
+                device_id_type=MESH,
+            )
+            copy.start()
+            copies.append(copy)
+        meanwhile()
+        for offset, copy in enumerate(copies, 1):
+            copy.wait()
+            value = jnp.maximum(value, slots[offset])
+    alphas = [jnp.broadcast_to(value[d : d + 1], tile) for d in range(3)]
+
+    z_split([edge_ref[r] for r in range(NVAR)], 14)
+    lax.fori_loop(0, 8, z_own, 0)
+    lax.fori_loop(0, 9, z_faces, 0)
+
+    split_own(1, turn_ref, turned)
+    halos[2].wait()
+    halos[3].wait()
+    cells_halo(1, turn_ref, y_halo_tile)
     differences(13)
-    faces_across(1, fx_ref)
+    faces_across(1, turn_ref, fx_ref)
 
     def y_rate(y, _):
         for r in range(NVAR):
@@ -350,19 +443,12 @@
 
     lax.fori_loop(0, 8, y_rate, 0)
 
-    lax.fori_loop(0, 3, x_halo, 0)
-    lax.fori_loop(0, 8, x_own, 0)
+    split_own(0, prim_ref, own)
+    halos[0].wait()
+    halos[1].wait()
+    cells_halo(0, prim_ref, lambda side, r, k: hx_ref[side, r, k])
     differences(13)
-    faces_across(0, fx_ref)
-
-    for r in range(NVAR):
-        edge_ref[r] = jnp.zeros(tile, jnp.float32)
-    lax.fori_loop(0, 8, z_edge, 0)
-    edge = [edge_ref[r] for r in range(NVAR)]
-    fill_cells(edge, 11, table_ref, prim_ref)
-    z_split(edge, 11)
-    lax.fori_loop(0, 8, z_own, 0)
-    lax.fori_loop(0, 9, z_faces, 0)
+    faces_across(0, prim_ref, fx_ref)
 
     scale = (-COURANT / 6.0) / (alphas[0] + alphas[1] + alphas[2])
     near = jnp.where(lane < 2, lane + 3, lane - lanes + 13)
@@ -383,76 +469,53 @@
     lax.fori_loop(0, 8, finish, 0)
 
 
-def increment(nasa_table, gas_constant, species_index, kinds, speeds, flat, hx, hy):
-    lanes = flat.shape[1]
+def shards(preserved_vector, nasa_table, gas_constant, species_index, face_kind):
+    _, nx, ny, lanes = preserved_vector.shape
+    size_x, size_y = lax.axis_size("gx"), lax.axis_size("gy")
+    flat = preserved_vector.reshape(NVAR * nx * ny, lanes)
     smem = pl.BlockSpec(memory_space=pltpu.SMEM)
-    vmem = pl.BlockSpec(memory_space=pltpu.VMEM)
+    anywhere = pl.BlockSpec(memory_space=pl.ANY)
+    dma = pltpu.SemaphoreType.DMA
 
     def buffer(*shape):
         return pltpu.VMEM(shape + (8, lanes), jnp.float32)
 
-    return pl.pallas_call(
-        compute,
+    out = pl.pallas_call(
+        functools.partial(fused, size_x, size_y),
         out_shape=jax.ShapeDtypeStruct(flat.shape, jnp.float32),
-        in_specs=[smem] * 4 + [vmem] * 4,
-        out_specs=vmem,
+        in_specs=[smem] * 4 + [anywhere] * 3,
+        out_specs=pl.BlockSpec(memory_space=pltpu.VMEM),
         scratch_shapes=[
+            pltpu.VMEM(flat.shape, jnp.float32),
+            buffer(2, NVAR, 3),
+            pltpu.VMEM((2, NVAR, nx, 3, 1, lanes), jnp.float32),
+            buffer(),
+            buffer(),
+            buffer(size_y),
+            buffer(size_x),
             buffer(TABLE),
-            buffer(PRIMS + 1, 14),
-            buffer(NVAR + 1, 14),
-            buffer(NVAR + 1, 14),
-            buffer(NVAR + 1, 14),
-            buffer(NVAR + 1, 14),
+            buffer(PRIMS + 1, 15),
+            buffer(PRIMS + 1, 15),
+            buffer(NVAR + 1, 15),
+            buffer(NVAR + 1, 15),
+            buffer(NVAR + 1, 15),
+            buffer(NVAR + 1, 15),
             buffer(NVAR, 9),
             buffer(NVAR, 9),
             pltpu.VMEM(flat.shape, jnp.float32),
             buffer(NVAR),
+            dma(()),
+            dma((size_x + size_y,)),
+            dma((size_y,)),
+            dma((size_x,)),
+            dma((4,)),
+            dma((4,)),
         ],
+        compiler_params=pltpu.CompilerParams(collective_id=0, has_side_effects=True),
         name="increment",
-    )(nasa_table, gas_constant, species_index, kinds, speeds, flat, hx, hy)
-
-
-def speed_kernel(nasa_ref, gas_ref, index_ref, x_ref, out_ref, table_ref):
-    block = 64
-    fill_table(nasa_ref, gas_ref, index_ref, table_ref)
-
-    def step(x, best):
-        u = [x_ref[pl.ds(pl.multiple_of(r * block + x * 8, 8), 8), :] for r in range(NVAR)]
-        _, vel, _, _, _, _, sound = thermo(u, table_ref)
-        return tuple(jnp.maximum(b, jnp.abs(v) + sound) for b, v in zip(best, vel))
-
-    zero = jnp.zeros((8, x_ref.shape[1]), jnp.float32)
-    for d, value in enumerate(lax.fori_loop(0, 8, step, (zero, zero, zero))):
-        out_ref[d] = value
-
-
-def shards(preserved_vector, nasa_table, gas_constant, species_index, face_kind):
-    _, nx, ny, lanes = preserved_vector.shape
-    flat = preserved_vector.reshape(NVAR * nx * ny, lanes)
-    smem = pl.BlockSpec(memory_space=pltpu.SMEM)
-    vmem = pl.BlockSpec(memory_space=pltpu.VMEM)
-    local = pl.pallas_call(
-        speed_kernel,
-        out_shape=jax.ShapeDtypeStruct((3, 8, lanes), jnp.float32),
-        in_specs=[smem] * 3 + [vmem],
-        out_specs=vmem,
-        scratch_shapes=[pltpu.VMEM((TABLE, 8, lanes), jnp.float32)],
-        name="speeds",
-    )(nasa_table, gas_constant, species_index, flat)
-    speeds = lax.pmax(jnp.max(local, axis=(1, 2)), ("gx", "gy"))
-    speeds = jnp.broadcast_to(speeds[:, None, None], (3, 8, lanes))
-
-    def swap(low, high, axis):
-        n = lax.axis_size(axis)
-        ahead = [(i, (i + 1) % n) for i in range(n)]
-        back = [(b, a) for a, b in ahead]
-        return jnp.stack([lax.ppermute(high, axis, ahead), lax.ppermute(low, axis, back)])
-
-    hx = swap(preserved_vector[:, :3], preserved_vector[:, -3:], "gx")
-    turned = jnp.swapaxes(preserved_vector, 1, 2)
-    hy = swap(turned[:, :3], turned[:, -3:], "gy")
-    out = increment(
-        nasa_table, gas_constant, species_index, face_kind.reshape(2), speeds, flat, hx, hy
+    )(
+        nasa_table.T, gas_constant, species_index, face_kind.reshape(2), flat,
+        preserved_vector, preserved_vector.reshape(NVAR, nx, ny, 1, lanes),
     )
     return out.reshape(preserved_vector.shape)
 

time: 69.4 us -> 31.1 us (0.45)
  blocking collectives: 37.8 us -> 0 us
  Pallas kernels: 18.3 us -> 29.1 us
  starting transfers between devices: 7.95 us -> 0 us
  other arithmetic: 2.32 us -> 0 us
    pmax x1 -> x0, blocking collectives: 37.8 us -> none  [shards(): speeds = lax.pmax(jnp.max(local, axis=(1, 2)), ('gx', 'gy'))]
    pallas_call x2 -> x1, Pallas kernels: 18.3 us -> 29.1 us  [shards(): pl.pallas_call(functools.partial(fused, size_x, size_y), out_shape=jax.Sh...]
    ppermute x4 -> x0, starting transfers between devices: 7.95 us -> none  [the longest x2 5.08 us: swap(): lax.ppermute(low, axis, back)]
    another operation x2 -> x0, other arithmetic: 1.51 us -> none  [swap(): jnp.stack([lax.ppermute(high, axis, ahead), lax.ppermute(low, axis, back)])]
    reduce_max x1 -> x0, other arithmetic: 0.81 us -> none  [shards(): speeds = lax.pmax(jnp.max(local, axis=(1, 2)), ('gx', 'gy'))]
    unnamed x6 -> x1, local copies, waits for them, and re-layouts: 1.79 us -> 1.82 us
  transfers between devices with their start and end apart: 4 -> 0, of which waited for: 0 -> 0; matrix products, arithmetic and copies ran while one was open for 3% -> 0% of each run, Pallas kernels for 3% -> 0%
where the time goes in v3:
time: 31.1 us; the launch traced here: 30.9 us
  Pallas kernels  29.1 us (94%)
  local copies, waits for them, and re-layouts  1.82 us (6%)
    pallas_call x1, Pallas kernels, shards(): pl.pallas_call(functools.partial(fused, size_x, size_y), out_shape=jax.Sh...  29.1 us
    unnamed x1, local copies, waits for them, and re-layouts  1.82 us

profile of v3, /device:TPU:0, one launch (start us, length us, event | category | flops | bytes accessed | tf_op | source)
XLA Modules:
  0.0 30.9 jit_solution(15639391248741111141)
XLA Ops:
  0.0 29.1 %increment.1 = f32[896,128]{1,0:T(8,128)} custom-call(f32[6,32]{1,0:T(8,128)} %bitcast.8, f32[32]{0:T(128)} %gas_ref.1, s32[9]{0:T(128)} %index_ref.1, s32[2]{0:T(128)} %bitcast.9, f32[896,128]{1,0:T(8,128)} %bitcast.5, f32[14,8,8,128]{3,2,1,0:T(8,128)} %planes_ref.1, f32[14,8,8,1,128]{4,3,2,1,0:T(1,128)} %bitcast.6), custom_call_target="tpu_custom_call" | custom-call | tf_op jit(solution)/shard_map/increment/pallas_call | solution.py:483
  29.1 1.8 %copy.7 = f32[14,8,8,128]{3,2,1,0:T(8,128)} copy(f32[14,8,8,128]{3,2,1,0:T(8,128)} %bitcast.7) | data formatting | bytes 917504

commit v4 on v3

--- a/solution.py
+++ b/solution.py
@@ -201,7 +201,7 @@
     nasa_ref, gas_ref, index_ref, kind_ref, flat_ref, planes_ref, source_ref, out_ref,
     x_ref, hx_ref, hy_ref, mine_ref, line_ref, slots_y, slots_x,
     table_ref, prim_ref, turn_ref, up_ref, down_ref, dup_ref, ddown_ref,
-    fx_ref, fz_ref, acc_ref, edge_ref,
+    fx_ref, fz_ref, acc_ref, edge_ref, fy_ref, s0_ref, s1_ref, s2_ref, s3_ref,
     load_sem, small_send, recv_y, recv_x, big_send, big_recv,
 ):
     load = pltpu.make_async_copy(flat_ref, x_ref, load_sem)
@@ -253,16 +253,20 @@
     def turned(r, y):
         return x_ref[pl.ds(r * block + y, 8, stride=8), :]
 
-    def differences(count):
+    def differences(first, last, split):
+        up_ref, down_ref, dup_ref, ddown_ref = split
+
         def step(i, _):
             for k in range(NVAR + 1):
                 dup_ref[k, i] = up_ref[k, i + 1] - up_ref[k, i]
                 ddown_ref[k, i] = down_ref[k, i + 1] - down_ref[k, i]
             return 0
 
-        lax.fori_loop(0, count, step, 0)
-
-    def faces_across(normal, prim_ref, flux_ref):
+        lax.fori_loop(first, last, step, 0)
+
+    def faces_across(normal, first, last, prim_ref, split, flux_ref):
+        up_ref, down_ref, dup_ref, ddown_ref = split
+
         def step(i, _):
             def linear(r):
                 here = up_ref[r, i + 2] + down_ref[r, i + 3]
@@ -282,25 +286,25 @@
             )
             return 0
 
-        lax.fori_loop(0, 9, step, 0)
+        lax.fori_loop(first, last, step, 0)
 
     def y_halo_tile(side, r, k):
         return hy_ref[side, r, :, k, 0, :]
 
-    def cells_halo(normal, prims, read):
+    def cells_halo(normal, prims, split, read):
         def step(k, _):
             for side, base in ((0, 0), (1, 11)):
                 u = [read(side, r, k) for r in range(NVAR)]
                 fill_cells(u, k + base, table_ref, prims)
-                fill_split(u, k + base, normal, alphas[normal], prims, up_ref, down_ref)
+                fill_split(u, k + base, normal, alphas[normal], prims, *split[:2])
             return 0
 
         lax.fori_loop(0, 3, step, 0)
 
-    def split_own(normal, prims, read):
+    def split_own(normal, prims, split, read):
         def step(n, _):
             u = [read(r, n) for r in range(NVAR)]
-            fill_split(u, n + 3, normal, alphas[normal], prims, up_ref, down_ref)
+            fill_split(u, n + 3, normal, alphas[normal], prims, *split[:2])
             return 0
 
         lax.fori_loop(0, 8, step, 0)
@@ -429,26 +433,30 @@
     lax.fori_loop(0, 8, z_own, 0)
     lax.fori_loop(0, 9, z_faces, 0)
 
-    split_own(1, turn_ref, turned)
-    halos[2].wait()
-    halos[3].wait()
-    cells_halo(1, turn_ref, y_halo_tile)
-    differences(13)
-    faces_across(1, turn_ref, fx_ref)
+    splits = (up_ref, down_ref, dup_ref, ddown_ref), (s0_ref, s1_ref, s2_ref, s3_ref)
+    plans = (
+        (1, turn_ref, splits[1], turned, y_halo_tile, fy_ref, halos[2:]),
+        (0, prim_ref, splits[0], own, lambda side, r, k: hx_ref[side, r, k], fx_ref, halos[:2]),
+    )
+    for normal, prims, split, read, _, flux, _ in plans:
+        split_own(normal, prims, split, read)
+        differences(3, 10, split)
+        faces_across(normal, 3, 6, prims, split, flux)
+    for normal, prims, split, _, read, flux, copies in plans:
+        for copy in copies:
+            copy.wait()
+        cells_halo(normal, prims, split, read)
+        differences(0, 3, split)
+        differences(10, 13, split)
+        faces_across(normal, 0, 3, prims, split, flux)
+        faces_across(normal, 6, 9, prims, split, flux)
 
     def y_rate(y, _):
         for r in range(NVAR):
-            acc_ref[pl.ds(r * block + y, 8, stride=8), :] = fx_ref[r, y + 1] - fx_ref[r, y]
+            acc_ref[pl.ds(r * block + y, 8, stride=8), :] = fy_ref[r, y + 1] - fy_ref[r, y]
         return 0
 
     lax.fori_loop(0, 8, y_rate, 0)
-
-    split_own(0, prim_ref, own)
-    halos[0].wait()
-    halos[1].wait()
-    cells_halo(0, prim_ref, lambda side, r, k: hx_ref[side, r, k])
-    differences(13)
-    faces_across(0, prim_ref, fx_ref)
 
     scale = (-COURANT / 6.0) / (alphas[0] + alphas[1] + alphas[2])
     near = jnp.where(lane < 2, lane + 3, lane - lanes + 13)
@@ -504,6 +512,8 @@
             buffer(NVAR, 9),
             pltpu.VMEM(flat.shape, jnp.float32),
             buffer(NVAR),
+            buffer(NVAR, 9),
+            *[buffer(NVAR + 1, 15) for _ in range(4)],
             dma(()),
             dma((size_x + size_y,)),
             dma((size_y,)),

time: 31.1 us -> 31.1 us (level)
  no operation moved by 1% of the time
where the time goes in v4:
time: 31.1 us; the launch traced here: 30.9 us
  Pallas kernels  29.1 us (94%)
  local copies, waits for them, and re-layouts  1.82 us (6%)
    pallas_call x1, Pallas kernels, shards(): pl.pallas_call(functools.partial(fused, size_x, size_y), out_shape=jax.Sh...  29.1 us
    unnamed x1, local copies, waits for them, and re-layouts  1.82 us

profile of v4, /device:TPU:0, one launch (start us, length us, event | category | flops | bytes accessed | tf_op | source)
XLA Modules:
  0.0 30.9 jit_solution(9103034668623389379)
XLA Ops:
  0.0 29.1 %increment.1 = f32[896,128]{1,0:T(8,128)} custom-call(f32[6,32]{1,0:T(8,128)} %bitcast.8, f32[32]{0:T(128)} %gas_ref.1, s32[9]{0:T(128)} %index_ref.1, s32[2]{0:T(128)} %bitcast.9, f32[896,128]{1,0:T(8,128)} %bitcast.5, f32[14,8,8,128]{3,2,1,0:T(8,128)} %planes_ref.1, f32[14,8,8,1,128]{4,3,2,1,0:T(1,128)} %bitcast.6), custom_call_target="tpu_custom_call" | custom-call | tf_op jit(solution)/shard_map/increment/pallas_call | solution.py:491
  29.1 1.8 %copy.7 = f32[14,8,8,128]{3,2,1,0:T(8,128)} copy(f32[14,8,8,128]{3,2,1,0:T(8,128)} %bitcast.7) | data formatting | bytes 917504
